TPU v7x, 256 devices: a whole 4x4x8 slice. The times are simulated.
256 devices in a mesh: outer: 4 (over y_hi, core), inner: 64 (over y_lo, z, x).
Axes of the slice: x: 4, y: 4 (y_hi: 2, y_lo: 2; y = y_hi * 2 + y_lo), z: 8, core: 2. Of those that a mesh axis runs over, the one named last changes fastest.
Arguments:
- queries: bfloat16 [32768, 2048], P(('outer', 'inner')), may hold values from -2 to 2
- keys: bfloat16 [32768, 2048], P(('outer', 'inner')), may hold values from -2 to 2
- values: bfloat16 [32768, 2048], P(('outer', 'inner')), may hold values from -6 to 6
- grad_out: bfloat16 [32768, 2048], P(('outer', 'inner')), may hold values from -96 to 96
- window: int32 [1], replicated, may hold values from 513 to 640
Outputs:
- query_grad: bfloat16 [32768, 2048], P(('outer', 'inner'))
- key_grad: bfloat16 [32768, 2048], P(('outer', 'inner'))
- value_grad: bfloat16 [32768, 2048], P(('outer', 'inner'))
All inputs are finite; a program needn't handle non-finite values.
Results may differ from a plain program's by a relative error of at most 0.0085.
Values may be sent and summed in bfloat16 or wider, within the bound.
No kernel may reach another device: no remote copies, remote signals or barrier semaphores. Data moves between devices by JAX's collectives and lax.ppermute only.
A program may use at most 64 MiB of HBM per device.

v0:
```python
import jax
import jax.numpy as jnp
from jax import lax
from jax.sharding import PartitionSpec as P

HEADS = 16
HD = 128


def shifted(value, axis, steps):
    count = lax.axis_size(axis)
    first, last = (max(0, -steps), min(count, count - steps))
    return lax.ppermute(value, axis, [(source, source + steps) for source in range(first, last)])


def visible(query_start, key_start, count, width, total):
    query_pos = query_start + jnp.arange(count, dtype=jnp.int32)[:, None]
    key_pos = key_start + jnp.arange(count, dtype=jnp.int32)[None, :]
    return (
        (key_pos <= query_pos)
        & (key_pos > query_pos - width)
        & (key_pos >= 0)
        & (query_pos < total)
    )


def head_scores(query_block, key_block):
    return jnp.einsum(
        "qhd,khd->hqk", query_block, key_block, preferred_element_type=jnp.float32
    ) * HD ** (-0.5)


def pair_grads(query_block, out_grad, log_norm, centre, key_block, value_block, allowed):
    scale = HD ** (-0.5)
    logits = head_scores(query_block, key_block)
    probs = jnp.where(allowed[None], jnp.exp(logits - log_norm[:, :, None]), 0.0)
    probs_low = probs.astype(jnp.bfloat16)
    value_term = jnp.einsum("hqk,qhd->khd", probs_low, out_grad, preferred_element_type=jnp.float32)
    prob_grad = jnp.einsum(
        "qhd,khd->hqk", out_grad, value_block, preferred_element_type=jnp.float32
    )
    logit_grad = (probs * (prob_grad - centre[:, :, None])).astype(jnp.bfloat16)
    query_term = (
        jnp.einsum("hqk,khd->qhd", logit_grad, key_block, preferred_element_type=jnp.float32)
        * scale
    )
    key_term = (
        jnp.einsum("hqk,qhd->khd", logit_grad, query_block, preferred_element_type=jnp.float32)
        * scale
    )
    return (
        query_term.astype(jnp.bfloat16),
        key_term.astype(jnp.bfloat16),
        value_term.astype(jnp.bfloat16),
    )


def per_device(queries, keys, values, grad_out, window):
    count = queries.shape[0]
    total = lax.axis_size(("outer", "inner")) * count
    start = lax.axis_index(("outer", "inner")) * count
    width = window[0]
    shaped = (count, HEADS, HD)
    query_block = queries.reshape(shaped)
    key_block = keys.reshape(shaped)
    value_block = values.reshape(shaped)
    grad_block = grad_out.reshape(shaped)
    fetched = [(key_block, value_block)]
    passing = (key_block, value_block)
    for hop in range(1, 6):
        passing = shifted((passing[0], passing[1]), ("outer", "inner"), 1)
        fetched.append(passing)
    norm_total = jnp.zeros((HEADS, count), jnp.float32)
    weighted = jnp.zeros(shaped, jnp.float32)
    for hop in range(6):
        allowed = visible(start, start - hop * count, count, width, total)
        logits = head_scores(query_block, fetched[hop][0])
        weights = jnp.where(allowed[None], jnp.exp(logits), 0.0)
        norm_total = norm_total + jnp.sum(weights, axis=2)
        weighted = weighted + jnp.einsum(
            "hqk,khd->qhd",
            weights.astype(jnp.bfloat16),
            fetched[hop][1],
            preferred_element_type=jnp.float32,
        )
    log_norm = jnp.log(norm_total)
    output = weighted / jnp.transpose(norm_total)[:, :, None]
    centre = jnp.transpose(jnp.sum(grad_block.astype(jnp.float32) * output, axis=2))
    query_total = jnp.zeros(shaped, jnp.float32)
    key_total = jnp.zeros(shaped, jnp.float32)
    value_total = jnp.zeros(shaped, jnp.float32)
    for hop in range(6):
        if hop == 0:
            bundle = (query_block, grad_block, log_norm, centre)
        else:
            bundle = (
                shifted(query_block.astype(jnp.float32), ("outer", "inner"), -hop).astype(
                    query_block.dtype
                ),
                shifted(grad_block.astype(jnp.float32), ("outer", "inner"), -hop).astype(
                    grad_block.dtype
                ),
                shifted(log_norm, ("outer", "inner"), -hop),
                shifted(centre, ("outer", "inner"), -hop),
            )
        allowed = visible(start + hop * count, start, count, width, total)
        query_term, key_term, value_term = pair_grads(
            bundle[0], bundle[1], bundle[2], bundle[3], key_block, value_block, allowed
        )
        key_total = key_total + key_term.astype(jnp.float32)
        value_total = value_total + value_term.astype(jnp.float32)
        if hop == 0:
            query_total = query_term.astype(jnp.float32)
        else:
            returned = shifted(query_term, ("outer", "inner"), hop)
            query_total = query_total + returned.astype(jnp.float32)
    flat = (count, HEADS * HD)
    return (
        query_total.reshape(flat).astype(jnp.bfloat16),
        key_total.reshape(flat).astype(jnp.bfloat16),
        value_total.reshape(flat).astype(jnp.bfloat16),
    )


def solution(mesh):
    placed = (
        P(("outer", "inner"), None),
        P(("outer", "inner"), None),
        P(("outer", "inner"), None),
        P(("outer", "inner"), None),
        P(),
    )
    return jax.shard_map(
        per_device,
        mesh=mesh,
        in_specs=placed,
        out_specs=(
            P(("outer", "inner"), None),
            P(("outer", "inner"), None),
            P(("outer", "inner"), None),
        ),
        check_vma=False,
    )
```

profile of v0, /device:TPU:24, one launch (start us, length us, event | category | flops | bytes accessed | tf_op | source)
XLA Modules:
  0.0 301.5 jit_solution(2838616467589030881)
XLA Ops:
  3.0 10.6 %collective-permute-start.30 = (bf16[128,16,128]{2,0,1:T(8,128)(2,1)}, bf16[128,16,128]{2,0,1:T(8,128)(2,1)}, u32[]{:S(2)}, u32[]{:S(2)}) collective-permute-start(bf16[128,16,128]{2,0,1:T(8,128)(2,1)} %copy.94), channel_id=1, source_target_pairs={{5,0},{6,1},{7,2},{8,3},{9,4},{10,5},{11,6},{12,7},{13,8},{14,9},{... | collective-permute-start | bytes 1572872 | tf_op jit(solution)/shard_map/ppermute | solution.py:13
  22.6 6.2 %collective-permute-start.32 = (bf16[128,16,128]{0,2,1:T(8,128)(2,1)S(1)}, bf16[128,16,128]{0,2,1:T(8,128)(2,1)S(1)}, u32[]{:S(2)}, u32[]{:S(2)}) collective-permute-start(bf16[128,16,128]{0,2,1:T(8,128)(2,1)S(1)} %bitcast.145), channel_id=1, source_target_pairs={{5,0},{6,1},{7,2},{8,3},{9,4},{10,5},{11,6},{12,7},{13,8},{14,9},{... | collective-permute-start | bytes 1572872 | tf_op jit(solution)/shard_map/ppermute | solution.py:13
  30.9 8.3 %collective-permute-done = bf16[128,16,128]{2,0,1:T(8,128)(2,1)} collective-permute-done((bf16[128,16,128]{2,0,1:T(8,128)(2,1)}, bf16[128,16,128]{2,0,1:T(8,128)(2,1)}, u32[]{:S(2)}, u32[]{:S(2)}) %collective-permute-start) | collective-permute-done | bytes 524320 | tf_op jit(solution)/shard_map/ppermute | solution.py:13
  41.0 9.3 %collective-permute-done.5 = bf16[128,16,128]{0,2,1:T(8,128)(2,1)} collective-permute-done((bf16[128,16,128]{0,2,1:T(8,128)(2,1)S(1)}, bf16[128,16,128]{0,2,1:T(8,128)(2,1)}, u32[]{:S(2)}, u32[]{:S(2)}) %collective-permute-start.5) | collective-permute-done | bytes 524320 | tf_op jit(solution)/shard_map/ppermute | solution.py:13
  55.1 6.4 %collective-permute-done.1 = bf16[128,16,128]{2,0,1:T(8,128)(2,1)S(1)} collective-permute-done((bf16[128,16,128]{2,0,1:T(8,128)(2,1)}, bf16[128,16,128]{2,0,1:T(8,128)(2,1)S(1)}, u32[]{:S(2)}, u32[]{:S(2)}) %collective-permute-start.1) | collective-permute-done | bytes 524320 | tf_op jit(solution)/shard_map/ppermute | solution.py:13
  63.4 9.3 %collective-permute-done.6 = bf16[128,16,128]{0,2,1:T(8,128)(2,1)S(1)} collective-permute-done((bf16[128,16,128]{0,2,1:T(8,128)(2,1)}, bf16[128,16,128]{0,2,1:T(8,128)(2,1)S(1)}, u32[]{:S(2)}, u32[]{:S(2)}) %collective-permute-start.6) | collective-permute-done | bytes 524320 | tf_op jit(solution)/shard_map/ppermute | solution.py:13
  75.4 8.6 %collective-permute-done.2 = bf16[128,16,128]{2,0,1:T(8,128)(2,1)S(1)} collective-permute-done((bf16[128,16,128]{2,0,1:T(8,128)(2,1)S(1)}, bf16[128,16,128]{2,0,1:T(8,128)(2,1)S(1)}, u32[]{:S(2)}, u32[]{:S(2)}) %collective-permute-start.2) | collective-permute-done | bytes 524320 | tf_op jit(solution)/shard_map/ppermute | solution.py:13
  85.9 9.3 %collective-permute-done.7 = bf16[128,16,128]{0,2,1:T(8,128)(2,1)S(1)} collective-permute-done((bf16[128,16,128]{0,2,1:T(8,128)(2,1)S(1)}, bf16[128,16,128]{0,2,1:T(8,128)(2,1)S(1)}, u32[]{:S(2)}, u32[]{:S(2)}) %collective-permute-start.7) | collective-permute-done | bytes 524320 | tf_op jit(solution)/shard_map/ppermute | solution.py:13
  97.9 8.6 %collective-permute-done.3 = bf16[128,16,128]{2,0,1:T(8,128)(2,1)S(1)} collective-permute-done((bf16[128,16,128]{2,0,1:T(8,128)(2,1)S(1)}, bf16[128,16,128]{2,0,1:T(8,128)(2,1)S(1)}, u32[]{:S(2)}, u32[]{:S(2)}) %collective-permute-start.3) | collective-permute-done | bytes 524320 | tf_op jit(solution)/shard_map/ppermute | solution.py:13
  108.4 9.3 %collective-permute-done.8 = bf16[128,16,128]{0,2,1:T(8,128)(2,1)S(1)} collective-permute-done((bf16[128,16,128]{0,2,1:T(8,128)(2,1)S(1)}, bf16[128,16,128]{0,2,1:T(8,128)(2,1)S(1)}, u32[]{:S(2)}, u32[]{:S(2)}) %collective-permute-start.8) | collective-permute-done | bytes 524320 | tf_op jit(solution)/shard_map/ppermute | solution.py:13
  120.3 8.6 %collective-permute-done.4 = bf16[128,16,128]{2,0,1:T(8,128)(2,1)S(1)} collective-permute-done((bf16[128,16,128]{2,0,1:T(8,128)(2,1)S(1)}, bf16[128,16,128]{2,0,1:T(8,128)(2,1)S(1)}, u32[]{:S(2)}, u32[]{:S(2)}) %collective-permute-start.4) | collective-permute-done | bytes 524320 | tf_op jit(solution)/shard_map/ppermute | solution.py:13
  131.3 7.2 %collective-permute-done.9 = bf16[128,16,128]{0,2,1:T(8,128)(2,1)S(1)} collective-permute-done((bf16[128,16,128]{0,2,1:T(8,128)(2,1)S(1)}, bf16[128,16,128]{0,2,1:T(8,128)(2,1)S(1)}, u32[]{:S(2)}, u32[]{:S(2)}) %collective-permute-start.9) | collective-permute-done | bytes 524320 | tf_op jit(solution)/shard_map/ppermute | solution.py:13
  145.2 5.9 %collective-permute-start.33 = (f32[16,128]{1,0:T(8,128)S(1)}, f32[16,128]{1,0:T(8,128)S(1)}, u32[]{:S(2)}, u32[]{:S(2)}) collective-permute-start(f32[16,128]{1,0:T(8,128)S(1)} %bitcast.158), channel_id=1, source_target_pairs={{5,0},{6,1},{7,2},{8,3},{9,4},{10,5},{11,6},{12,7},{13,8},{14,9},{... | collective-permute-start | bytes 24584 | tf_op jit(solution)/shard_map/ppermute | solution.py:13
  154.6 6.5 %collective-permute-done.33 = f32[16,128]{1,0:T(8,128)S(1)} collective-permute-done((f32[16,128]{1,0:T(8,128)S(1)}, f32[16,128]{1,0:T(8,128)S(1)}, u32[]{:S(2)}, u32[]{:S(2)}) %collective-permute-start.33) | collective-permute-done | bytes 8224 | tf_op jit(solution)/shard_map/ppermute | solution.py:13
  166.4 5.2 %collective-permute-done.26 = f32[16,128]{1,0:T(8,128)S(1)} collective-permute-done((f32[16,128]{1,0:T(8,128)S(1)}, f32[16,128]{1,0:T(8,128)S(1)}, u32[]{:S(2)}, u32[]{:S(2)}) %collective-permute-start.26) | collective-permute-done | bytes 8224 | tf_op jit(solution)/shard_map/ppermute | solution.py:13
  171.6 4.3 %collective-permute-start.28 = (f32[16,128]{1,0:T(8,128)S(1)}, f32[16,128]{1,0:T(8,128)S(1)}, u32[]{:S(2)}, u32[]{:S(2)}) collective-permute-start(f32[16,128]{1,0:T(8,128)S(1)} %bitcast.159), channel_id=1, source_target_pairs={{4,0},{5,1},{6,2},{7,3},{8,4},{9,5},{10,6},{11,7},{12,8},{13,9},{1... | collective-permute-start | bytes 24584 | tf_op jit(solution)/shard_map/ppermute | solution.py:13
  183.1 5.0 %collective-permute-start.21 = (f32[16,128]{1,0:T(8,128)S(1)}, f32[16,128]{1,0:T(8,128)S(1)}, u32[]{:S(2)}, u32[]{:S(2)}) collective-permute-start(f32[16,128]{1,0:T(8,128)S(1)} %get-tuple-element.9), channel_id=1, source_target_pairs={{3,0},{4,1},{5,2},{6,3},{7,4},{8,5},{9,6},{10,7},{11,8},{12,9},{13... | collective-permute-start | bytes 24584 | tf_op jit(solution)/shard_map/ppermute | solution.py:13
  188.5 3.8 %collective-permute-start.10 = (bf16[128,16,128]{2,0,1:T(8,128)(2,1)}, bf16[128,16,128]{2,0,1:T(8,128)(2,1)S(1)}, u32[]{:S(2)}, u32[]{:S(2)}) collective-permute-start(bf16[128,16,128]{2,0,1:T(8,128)(2,1)} %copy.94), channel_id=1, source_target_pairs={{1,0},{2,1},{3,2},{4,3},{5,4},{6,5},{7,6},{8,7},{9,8},{10,9},{11,1... | collective-permute-start | bytes 1572872 | tf_op jit(solution)/shard_map/ppermute | solution.py:13
  192.6 6.9 %collective-permute-start.23 = (f32[16,128]{1,0:T(8,128)S(1)}, f32[16,128]{1,0:T(8,128)S(1)}, u32[]{:S(2)}, u32[]{:S(2)}) collective-permute-start(f32[16,128]{1,0:T(8,128)S(1)} %bitcast.160), channel_id=1, source_target_pairs={{3,0},{4,1},{5,2},{6,3},{7,4},{8,5},{9,6},{10,7},{11,8},{12,9},{13... | collective-permute-start | bytes 24584 | tf_op jit(solution)/shard_map/ppermute | solution.py:13
  212.9 6.9 %collective-permute-start.11 = (f32[16,128]{1,0:T(8,128)S(1)}, f32[16,128]{1,0:T(8,128)S(1)}, u32[]{:S(2)}, u32[]{:S(2)}) collective-permute-start(f32[16,128]{1,0:T(8,128)S(1)} %get-tuple-element.9), channel_id=1, source_target_pairs={{1,0},{2,1},{3,2},{4,3},{5,4},{6,5},{7,6},{8,7},{9,8},{10,9},{11,1... | collective-permute-start | bytes 24584 | tf_op jit(solution)/shard_map/ppermute | solution.py:13
  221.3 4.5 %collective-permute-start.13 = (f32[16,128]{1,0:T(8,128)S(1)}, f32[16,128]{1,0:T(8,128)S(1)}, u32[]{:S(2)}, u32[]{:S(2)}) collective-permute-start(f32[16,128]{1,0:T(8,128)S(1)} %bitcast.162), channel_id=1, source_target_pairs={{1,0},{2,1},{3,2},{4,3},{5,4},{6,5},{7,6},{8,7},{9,8},{10,9},{11,1... | collective-permute-start | bytes 24584 | tf_op jit(solution)/shard_map/ppermute | solution.py:13
  232.7 6.1 %collective-permute-start.24 = (bf16[128,16,128]{0,2,1:T(8,128)(2,1)}, bf16[128,16,128]{0,2,1:T(8,128)(2,1)}, u32[]{:S(2)}, u32[]{:S(2)}) collective-permute-start(bf16[128,16,128]{0,2,1:T(8,128)(2,1)} %fusion.79), channel_id=1, source_target_pairs={{0,3},{1,4},{2,5},{3,6},{4,7},{5,8},{6,9},{7,10},{8,11},{9,12},{10... | collective-permute-start | bytes 1572872 | tf_op jit(solution)/shard_map/ppermute | solution.py:13
  262.7 14.6 %collective-permute-done.24 = bf16[128,16,128]{0,2,1:T(8,128)(2,1)} collective-permute-done((bf16[128,16,128]{0,2,1:T(8,128)(2,1)}, bf16[128,16,128]{0,2,1:T(8,128)(2,1)}, u32[]{:S(2)}, u32[]{:S(2)}) %collective-permute-start.24) | collective-permute-done | bytes 524320 | tf_op jit(solution)/shard_map/ppermute | solution.py:13
  279.6 18.7 %collective-permute-done.14 = bf16[128,16,128]{0,2,1:T(8,128)(2,1)} collective-permute-done((bf16[128,16,128]{0,2,1:T(8,128)(2,1)}, bf16[128,16,128]{0,2,1:T(8,128)(2,1)}, u32[]{:S(2)}, u32[]{:S(2)}) %collective-permute-start.14) | collective-permute-done | bytes 524320 | tf_op jit(solution)/shard_map/ppermute | solution.py:13
  (128 shorter events, 109.3 us)
Async XLA Ops:
  3.0 140.2 %collective-permute-start.30 = (bf16[128,16,128]{2,0,1:T(8,128)(2,1)}, bf16[128,16,128]{2,0,1:T(8,128)(2,1)}, u32[]{:S(2)}, u32[]{:S(2)}) collective-permute-start(bf16[128,16,128]{2,0,1:T(8,128)(2,1)} %copy.94), channel_id=1, source_target_pairs={{5,0},{6,1},{7,2},{8,3},{9,4},{10,5},{11,6},{12,7},{13,8},{14,9},{... | collective-permute-start | bytes 1572872 | tf_op jit(solution)/shard_map/ppermute | solution.py:13
  13.5 150.9 %collective-permute-start.25 = (bf16[128,16,128]{2,0,1:T(8,128)(2,1)}, bf16[128,16,128]{2,0,1:T(8,128)(2,1)}, u32[]{:S(2)}, u32[]{:S(2)}) collective-permute-start(bf16[128,16,128]{2,0,1:T(8,128)(2,1)} %copy.94), channel_id=1, source_target_pairs={{4,0},{5,1},{6,2},{7,3},{8,4},{9,5},{10,6},{11,7},{12,8},{13,9},{1... | collective-permute-start | bytes 1572872 | tf_op jit(solution)/shard_map/ppermute | solution.py:13
  17.8 21.3 %collective-permute-start = (bf16[128,16,128]{2,0,1:T(8,128)(2,1)}, bf16[128,16,128]{2,0,1:T(8,128)(2,1)}, u32[]{:S(2)}, u32[]{:S(2)}) collective-permute-start(bf16[128,16,128]{2,0,1:T(8,128)(2,1)} %copy.76), channel_id=1, source_target_pairs={{0,1},{1,2},{2,3},{3,4},{4,5},{5,6},{6,7},{7,8},{8,9},{9,10},{10,1... | collective-permute-start | bytes 1572872 | tf_op jit(solution)/shard_map/ppermute | solution.py:13
  20.1 30.2 %collective-permute-start.5 = (bf16[128,16,128]{0,2,1:T(8,128)(2,1)S(1)}, bf16[128,16,128]{0,2,1:T(8,128)(2,1)}, u32[]{:S(2)}, u32[]{:S(2)}) collective-permute-start(bf16[128,16,128]{0,2,1:T(8,128)(2,1)S(1)} %bitcast.129), channel_id=1, source_target_pairs={{0,1},{1,2},{2,3},{3,4},{4,5},{5,6},{6,7},{7,8},{8,9},{9,10},{10,1... | collective-permute-start | bytes 1572872 | tf_op jit(solution)/shard_map/ppermute | solution.py:13
  22.6 130.1 %collective-permute-start.32 = (bf16[128,16,128]{0,2,1:T(8,128)(2,1)S(1)}, bf16[128,16,128]{0,2,1:T(8,128)(2,1)S(1)}, u32[]{:S(2)}, u32[]{:S(2)}) collective-permute-start(bf16[128,16,128]{0,2,1:T(8,128)(2,1)S(1)} %bitcast.145), channel_id=1, source_target_pairs={{5,0},{6,1},{7,2},{8,3},{9,4},{10,5},{11,6},{12,7},{13,8},{14,9},{... | collective-permute-start | bytes 1572872 | tf_op jit(solution)/shard_map/ppermute | solution.py:13
  39.1 22.4 %collective-permute-start.1 = (bf16[128,16,128]{2,0,1:T(8,128)(2,1)}, bf16[128,16,128]{2,0,1:T(8,128)(2,1)S(1)}, u32[]{:S(2)}, u32[]{:S(2)}) collective-permute-start(bf16[128,16,128]{2,0,1:T(8,128)(2,1)} %collective-permute-done), channel_id=1, source_target_pairs={{0,1},{1,2},{2,3},{3,4},{4,5},{5,6},{6,7},{7,8},{8,9},{9,10},{10,1... | collective-permute-start | bytes 1572872 | tf_op jit(solution)/shard_map/ppermute | solution.py:13
  50.4 22.4 %collective-permute-start.6 = (bf16[128,16,128]{0,2,1:T(8,128)(2,1)}, bf16[128,16,128]{0,2,1:T(8,128)(2,1)S(1)}, u32[]{:S(2)}, u32[]{:S(2)}) collective-permute-start(bf16[128,16,128]{0,2,1:T(8,128)(2,1)} %collective-permute-done.5), channel_id=1, source_target_pairs={{0,1},{1,2},{2,3},{3,4},{4,5},{5,6},{6,7},{7,8},{8,9},{9,10},{10,1... | collective-permute-start | bytes 1572872 | tf_op jit(solution)/shard_map/ppermute | solution.py:13
  61.5 22.5 %collective-permute-start.2 = (bf16[128,16,128]{2,0,1:T(8,128)(2,1)S(1)}, bf16[128,16,128]{2,0,1:T(8,128)(2,1)S(1)}, u32[]{:S(2)}, u32[]{:S(2)}) collective-permute-start(bf16[128,16,128]{2,0,1:T(8,128)(2,1)S(1)} %collective-permute-done.1), channel_id=1, source_target_pairs={{0,1},{1,2},{2,3},{3,4},{4,5},{5,6},{6,7},{7,8},{8,9},{9,10},{10,1... | collective-permute-start | bytes 1572872 | tf_op jit(solution)/shard_map/ppermute | solution.py:13
  72.7 22.5 %collective-permute-start.7 = (bf16[128,16,128]{0,2,1:T(8,128)(2,1)S(1)}, bf16[128,16,128]{0,2,1:T(8,128)(2,1)S(1)}, u32[]{:S(2)}, u32[]{:S(2)}) collective-permute-start(bf16[128,16,128]{0,2,1:T(8,128)(2,1)S(1)} %collective-permute-done.6), channel_id=1, source_target_pairs={{0,1},{1,2},{2,3},{3,4},{4,5},{5,6},{6,7},{7,8},{8,9},{9,10},{10,1... | collective-permute-start | bytes 1572872 | tf_op jit(solution)/shard_map/ppermute | solution.py:13
  84.0 22.5 %collective-permute-start.3 = (bf16[128,16,128]{2,0,1:T(8,128)(2,1)S(1)}, bf16[128,16,128]{2,0,1:T(8,128)(2,1)S(1)}, u32[]{:S(2)}, u32[]{:S(2)}) collective-permute-start(bf16[128,16,128]{2,0,1:T(8,128)(2,1)S(1)} %collective-permute-done.2), channel_id=1, source_target_pairs={{0,1},{1,2},{2,3},{3,4},{4,5},{5,6},{6,7},{7,8},{8,9},{9,10},{10,1... | collective-permute-start | bytes 1572872 | tf_op jit(solution)/shard_map/ppermute | solution.py:13
  95.2 22.5 %collective-permute-start.8 = (bf16[128,16,128]{0,2,1:T(8,128)(2,1)S(1)}, bf16[128,16,128]{0,2,1:T(8,128)(2,1)S(1)}, u32[]{:S(2)}, u32[]{:S(2)}) collective-permute-start(bf16[128,16,128]{0,2,1:T(8,128)(2,1)S(1)} %collective-permute-done.7), channel_id=1, source_target_pairs={{0,1},{1,2},{2,3},{3,4},{4,5},{5,6},{6,7},{7,8},{8,9},{9,10},{10,1... | collective-permute-start | bytes 1572872 | tf_op jit(solution)/shard_map/ppermute | solution.py:13
  106.4 22.5 %collective-permute-start.4 = (bf16[128,16,128]{2,0,1:T(8,128)(2,1)S(1)}, bf16[128,16,128]{2,0,1:T(8,128)(2,1)S(1)}, u32[]{:S(2)}, u32[]{:S(2)}) collective-permute-start(bf16[128,16,128]{2,0,1:T(8,128)(2,1)S(1)} %collective-permute-done.3), channel_id=1, source_target_pairs={{0,1},{1,2},{2,3},{3,4},{4,5},{5,6},{6,7},{7,8},{8,9},{9,10},{10,1... | collective-permute-start | bytes 1572872 | tf_op jit(solution)/shard_map/ppermute | solution.py:13
  128.9 48.6 %collective-permute-start.27 = (bf16[128,16,128]{0,2,1:T(8,128)(2,1)S(1)}, bf16[128,16,128]{0,2,1:T(8,128)(2,1)S(1)}, u32[]{:S(2)}, u32[]{:S(2)}) collective-permute-start(bf16[128,16,128]{0,2,1:T(8,128)(2,1)S(1)} %bitcast.146), channel_id=1, source_target_pairs={{4,0},{5,1},{6,2},{7,3},{8,4},{9,5},{10,6},{11,7},{12,8},{13,9},{1... | collective-permute-start | bytes 1572872 | tf_op jit(solution)/shard_map/ppermute | solution.py:13
  143.2 45.3 %collective-permute-start.20 = (bf16[128,16,128]{2,0,1:T(8,128)(2,1)}, bf16[128,16,128]{2,0,1:T(8,128)(2,1)S(1)}, u32[]{:S(2)}, u32[]{:S(2)}) collective-permute-start(bf16[128,16,128]{2,0,1:T(8,128)(2,1)} %copy.94), channel_id=1, source_target_pairs={{3,0},{4,1},{5,2},{6,3},{7,4},{8,5},{9,6},{10,7},{11,8},{12,9},{13... | collective-permute-start | bytes 1572872 | tf_op jit(solution)/shard_map/ppermute | solution.py:13
  152.7 47.3 %collective-permute-start.22 = (bf16[128,16,128]{0,2,1:T(8,128)(2,1)S(1)}, bf16[128,16,128]{0,2,1:T(8,128)(2,1)S(1)}, u32[]{:S(2)}, u32[]{:S(2)}) collective-permute-start(bf16[128,16,128]{0,2,1:T(8,128)(2,1)S(1)} %bitcast.150), channel_id=1, source_target_pairs={{3,0},{4,1},{5,2},{6,3},{7,4},{8,5},{9,6},{10,7},{11,8},{12,9},{13... | collective-permute-start | bytes 1572872 | tf_op jit(solution)/shard_map/ppermute | solution.py:13
  164.4 43.0 %collective-permute-start.15 = (bf16[128,16,128]{2,0,1:T(8,128)(2,1)}, bf16[128,16,128]{2,0,1:T(8,128)(2,1)S(1)}, u32[]{:S(2)}, u32[]{:S(2)}) collective-permute-start(bf16[128,16,128]{2,0,1:T(8,128)(2,1)} %copy.94), channel_id=1, source_target_pairs={{2,0},{3,1},{4,2},{5,3},{6,4},{7,5},{8,6},{9,7},{10,8},{11,9},{12,... | collective-permute-start | bytes 1572872 | tf_op jit(solution)/shard_map/ppermute | solution.py:13
  177.5 43.8 %collective-permute-start.17 = (bf16[128,16,128]{0,2,1:T(8,128)(2,1)S(1)}, bf16[128,16,128]{0,2,1:T(8,128)(2,1)S(1)}, u32[]{:S(2)}, u32[]{:S(2)}) collective-permute-start(bf16[128,16,128]{0,2,1:T(8,128)(2,1)S(1)} %bitcast.151), channel_id=1, source_target_pairs={{2,0},{3,1},{4,2},{5,3},{6,4},{7,5},{8,6},{9,7},{10,8},{11,9},{12,... | collective-permute-start | bytes 1572872 | tf_op jit(solution)/shard_map/ppermute | solution.py:13
  188.5 42.0 %collective-permute-start.10 = (bf16[128,16,128]{2,0,1:T(8,128)(2,1)}, bf16[128,16,128]{2,0,1:T(8,128)(2,1)S(1)}, u32[]{:S(2)}, u32[]{:S(2)}) collective-permute-start(bf16[128,16,128]{2,0,1:T(8,128)(2,1)} %copy.94), channel_id=1, source_target_pairs={{1,0},{2,1},{3,2},{4,3},{5,4},{6,5},{7,6},{8,7},{9,8},{10,9},{11,1... | collective-permute-start | bytes 1572872 | tf_op jit(solution)/shard_map/ppermute | solution.py:13
  200.0 40.4 %collective-permute-start.12 = (bf16[128,16,128]{0,2,1:T(8,128)(2,1)S(1)}, bf16[128,16,128]{0,2,1:T(8,128)(2,1)S(1)}, u32[]{:S(2)}, u32[]{:S(2)}) collective-permute-start(bf16[128,16,128]{0,2,1:T(8,128)(2,1)S(1)} %bitcast.152), channel_id=1, source_target_pairs={{1,0},{2,1},{3,2},{4,3},{5,4},{6,5},{7,6},{8,7},{9,8},{10,9},{11,1... | collective-permute-start | bytes 1572872 | tf_op jit(solution)/shard_map/ppermute | solution.py:13
  225.9 36.9 %collective-permute-start.34 = (bf16[128,16,128]{0,2,1:T(8,128)(2,1)}, bf16[128,16,128]{0,2,1:T(8,128)(2,1)}, u32[]{:S(2)}, u32[]{:S(2)}) collective-permute-start(bf16[128,16,128]{0,2,1:T(8,128)(2,1)} %fusion.77), channel_id=1, source_target_pairs={{0,5},{1,6},{2,7},{3,8},{4,9},{5,10},{6,11},{7,12},{8,13},{9,14},{... | collective-permute-start | bytes 1572872 | tf_op jit(solution)/shard_map/ppermute | solution.py:13
  230.4 32.3 %collective-permute-start.29 = (bf16[128,16,128]{0,2,1:T(8,128)(2,1)}, bf16[128,16,128]{0,2,1:T(8,128)(2,1)}, u32[]{:S(2)}, u32[]{:S(2)}) collective-permute-start(bf16[128,16,128]{0,2,1:T(8,128)(2,1)} %fusion.78), channel_id=1, source_target_pairs={{0,4},{1,5},{2,6},{3,7},{4,8},{5,9},{6,10},{7,11},{8,12},{9,13},{1... | collective-permute-start | bytes 1572872 | tf_op jit(solution)/shard_map/ppermute | solution.py:13
  232.7 44.7 %collective-permute-start.24 = (bf16[128,16,128]{0,2,1:T(8,128)(2,1)}, bf16[128,16,128]{0,2,1:T(8,128)(2,1)}, u32[]{:S(2)}, u32[]{:S(2)}) collective-permute-start(bf16[128,16,128]{0,2,1:T(8,128)(2,1)} %fusion.79), channel_id=1, source_target_pairs={{0,3},{1,4},{2,5},{3,6},{4,7},{5,8},{6,9},{7,10},{8,11},{9,12},{10... | collective-permute-start | bytes 1572872 | tf_op jit(solution)/shard_map/ppermute | solution.py:13
  240.4 39.2 %collective-permute-start.19 = (bf16[128,16,128]{0,2,1:T(8,128)(2,1)}, bf16[128,16,128]{0,2,1:T(8,128)(2,1)}, u32[]{:S(2)}, u32[]{:S(2)}) collective-permute-start(bf16[128,16,128]{0,2,1:T(8,128)(2,1)} %fusion.80), channel_id=1, source_target_pairs={{0,2},{1,3},{2,4},{3,5},{4,6},{5,7},{6,8},{7,9},{8,10},{9,11},{10,... | collective-permute-start | bytes 1572872 | tf_op jit(solution)/shard_map/ppermute | solution.py:13
  243.8 54.5 %collective-permute-start.14 = (bf16[128,16,128]{0,2,1:T(8,128)(2,1)}, bf16[128,16,128]{0,2,1:T(8,128)(2,1)}, u32[]{:S(2)}, u32[]{:S(2)}) collective-permute-start(bf16[128,16,128]{0,2,1:T(8,128)(2,1)} %fusion.81), channel_id=1, source_target_pairs={{0,1},{1,2},{2,3},{3,4},{4,5},{5,6},{6,7},{7,8},{8,9},{9,10},{10,1... | collective-permute-start | bytes 1572872 | tf_op jit(solution)/shard_map/ppermute | solution.py:13
  (18 other events, 192.6 us)
where the time goes:
time: 303 us; the launch traced here: 302 us
  waiting for transfers between devices  141 us (47%)
  starting transfers between devices  114 us (38%)
  matrix products  36.7 us (12%)
  local copies, waits for them, and re-layouts  7.74 us (3%)
    ppermute x35, waiting for transfers between devices, shifted(): lax.ppermute(value, axis, [(source, source + steps) for source in range(f...  141 us
    ppermute x35, starting transfers between devices, shifted(): lax.ppermute(value, axis, [(source, source + steps) for source in range(f...  114 us
    dot_general x6, matrix products, pair_grads(): jnp.einsum('hqk,qhd->khd', probs_low, out_grad, preferred_element_type=jn...  10.4 us
    dot_general x11, matrix products, head_scores(): jnp.einsum('qhd,khd->hqk', query_block, key_block, preferred_element_type...  8.23 us
    dot_general x6, matrix products, pair_grads(): jnp.einsum('hqk,khd->qhd', logit_grad, key_block, preferred_element_type=...  7.84 us
  transfers between devices with their start and end apart: 35, of which 19 were waited for; matrix products, arithmetic and copies ran while one was open for 13% of the time, Pallas kernels for 0%

commit v1 on v0

v1 whole, which is shorter than its diff:
```python
import functools
import math

import jax
import jax.numpy as jnp
import numpy as np
from jax import lax
from jax.experimental import pallas as pl
from jax.experimental.pallas import tpu as pltpu
from jax.sharding import Mesh
from jax.sharding import PartitionSpec as P

HEADS = 16
HD = 128
BLK = 128
SIDE = 4
HH = HEADS // SIDE
SCALE = HD ** (-0.5)
SCALE2 = SCALE * math.log2(math.e)
OFF = -1e30
SEQ = ("o", "yl", "z")

NT = (((1,), (1,)), ((), ()))
NN = (((1,), (0,)), ((), ()))


def dot(a, b, dims):
    return lax.dot_general(a, b, dims, preferred_element_type=jnp.float32)


def tiles(width, axis):
    key = lax.broadcasted_iota(jnp.int32, (BLK, BLK), axis)
    query = lax.broadcasted_iota(jnp.int32, (BLK, BLK), 1 - axis)
    back = query - key
    zero = jnp.zeros((BLK, BLK), jnp.float32)
    return {
        0: jnp.where(back >= 0, zero, OFF),
        4: jnp.where(back + 4 * BLK < width, zero, OFF),
        5: jnp.where(back + 5 * BLK < width, zero, OFF),
    }


def query_kernel(scal, qg, kv, kvp, kvpp, dq, stats, cols, bias):
    width, has1, has2 = scal[0], scal[1], scal[2]
    for at, (_, tile) in enumerate(sorted(tiles(width, 1).items())):
        bias[at] = tile
    cols[...] = jnp.zeros_like(cols)
    lane = lax.broadcasted_iota(jnp.int32, (BLK, BLK), 1)
    off1 = jnp.where(has1 > 0, 0.0, OFF).astype(jnp.float32)
    off2 = jnp.where(has2 > 0, 0.0, OFF).astype(jnp.float32)

    def block(at, which, h):
        if at == 0:
            return kvpp[which, h]
        if at < 5:
            return kvp[at - 1, which, h]
        return kv[at - 5, which, h]

    def head(h, carry):
        for j in range(4):
            query = qg[j, 0, h]
            grad = qg[j, 1, h]
            weights, products = [], []
            norm = jnp.zeros((BLK, 1), jnp.float32)
            centre = jnp.zeros((BLK, 1), jnp.float32)
            for hop in range(6):
                at = j + 5 - hop
                logits = dot(query, block(at, 0, h), NT) * SCALE2
                if hop in (0, 4, 5):
                    logits = logits + bias[{0: 0, 4: 1, 5: 2}[hop]]
                if at < 5:
                    logits = logits + (off2 if at == 0 else off1)
                weight = jnp.exp2(logits)
                product = dot(grad, block(at, 1, h), NT)
                norm = norm + jnp.sum(weight, axis=1, keepdims=True)
                centre = centre + jnp.sum(weight * product, axis=1, keepdims=True)
                weights.append(weight)
                products.append(product)
            inverse = 1.0 / norm
            centre = centre * inverse
            total = jnp.zeros((BLK, HD), jnp.float32)
            for hop in range(6):
                at = j + 5 - hop
                change = (weights[hop] * inverse) * (products[hop] - centre)
                total = total + dot(change.astype(jnp.bfloat16), block(at, 0, h), NN)
            dq[j, h] = (total * SCALE).astype(jnp.bfloat16)
            row = j * 8 + h
            cols[...] = jnp.where(
                lane == row, jnp.log2(norm), jnp.where(lane == row + 4, centre, cols[...])
            )
        return carry

    lax.fori_loop(0, HH, head, 0)
    stats[...] = jnp.transpose(cols[...])[:32]


def key_pairs(j, h, hops, key, value, queries, stats_of, bias, dk, dv):
    for hop in hops:
        query, grad = queries(j + hop, h)
        log_norm, centre = stats_of(j + hop, h)
        logits = dot(key, query, NT) * SCALE2 - log_norm
        if hop in (0, 4, 5):
            logits = logits + bias[{0: 0, 4: 1, 5: 2}[hop]]
        probs = jnp.exp2(logits)
        product = dot(value, grad, NT)
        dv = dv + dot(probs.astype(jnp.bfloat16), grad, NN)
        change = probs * (product - centre)
        dk = dk + dot(change.astype(jnp.bfloat16), query, NN)
    return dk, dv


def own_key_kernel(scal, qg, kv, stats, part, bias):
    for at, (_, tile) in enumerate(sorted(tiles(scal[0], 0).items())):
        bias[at] = tile

    def stats_of(at, h):
        return stats[pl.ds(at * 8 + h, 1)], stats[pl.ds(at * 8 + 4 + h, 1)]

    def head(h, carry):
        for j in range(4):
            zero = jnp.zeros((BLK, HD), jnp.float32)
            dk, dv = key_pairs(
                j, h, range(0, 4 - j), kv[j, 0, h], kv[j, 1, h],
                lambda at, h: (qg[at, 0, h], qg[at, 1, h]), stats_of, bias, zero, zero,
            )
            part[j, 0, h] = dk
            part[j, 1, h] = dv
        return carry

    lax.fori_loop(0, HH, head, 0)


def far_key_kernel(scal, qgn, qgnn, kv, stats, far_stats, part, out, bias):
    for at, (_, tile) in enumerate(sorted(tiles(scal[0], 0).items())):
        bias[at] = tile

    def queries(at, h):
        if at == 8:
            return qgnn[0, h], qgnn[1, h]
        return qgn[at - 4, 0, h], qgn[at - 4, 1, h]

    def stats_of(at, h):
        if at == 8:
            return far_stats[pl.ds(h, 1)], far_stats[pl.ds(4 + h, 1)]
        row = (at - 4) * 8 + h
        return stats[pl.ds(row, 1)], stats[pl.ds(row + 4, 1)]

    def head(h, carry):
        for j in range(4):
            dk, dv = key_pairs(
                j, h, range(4 - j, 6), kv[j, 0, h], kv[j, 1, h],
                queries, stats_of, bias, part[j, 0, h], part[j, 1, h],
            )
            out[j, 0, h] = (dk * SCALE).astype(jnp.bfloat16)
            out[j, 1, h] = dv.astype(jnp.bfloat16)
        return carry

    lax.fori_loop(0, HH, head, 0)


def call(kernel, outs, scratch, *args):
    specs = [pl.BlockSpec(memory_space=pltpu.SMEM)]
    specs += [pl.BlockSpec(memory_space=pltpu.VMEM) for _ in args[1:]]
    return pl.pallas_call(
        kernel,
        out_shape=outs,
        in_specs=specs,
        out_specs=jax.tree.map(lambda _: pl.BlockSpec(memory_space=pltpu.VMEM), outs),
        scratch_shapes=scratch,
        compiler_params=pltpu.CompilerParams(vmem_limit_bytes=40 * 1024 * 1024),
    )(*args)


def shift(value, steps):
    count = lax.axis_size(SEQ)
    pairs = [(at, at + steps) for at in range(count) if 0 <= at + steps < count]
    return lax.ppermute(value, SEQ, pairs)


def spread(first, second):
    both = jnp.stack([first, second]).reshape(2, BLK, SIDE, HH, HD)
    return lax.all_to_all(jnp.transpose(both, (2, 0, 3, 1, 4)), "x", 0, 0)


def gather_back(blocks):
    mine = lax.all_to_all(blocks, "x", 0, 0)
    return mine


def flat(mine):
    return jnp.transpose(mine, (2, 0, 1, 3)).reshape(BLK, HEADS * HD)


def per_device(queries, keys, values, grad_out, window):
    f32 = jnp.float32
    group = lax.axis_index(SEQ)
    scal = jnp.stack(
        [window[0], (group >= 1).astype(jnp.int32), (group >= 2).astype(jnp.int32)]
    ).astype(jnp.int32)
    kv = spread(keys, values)
    last = shift(kv[3], 1)
    rest = shift(kv[:3], 1)
    kvpp = shift(last, 1)
    kvp = jnp.concatenate([rest, last[None]])
    qg = spread(queries, grad_out)
    head0 = shift(qg[0], -1)
    rest_q = shift(qg[1:], -1)
    qgnn = shift(head0, -1)
    qgn = jnp.concatenate([head0[None], rest_q])
    tile = (3, BLK, BLK)
    dq, stats = call(
        query_kernel,
        [
            jax.ShapeDtypeStruct((SIDE, HH, BLK, HD), jnp.bfloat16),
            jax.ShapeDtypeStruct((32, BLK), f32),
        ],
        [pltpu.VMEM((BLK, BLK), f32), pltpu.VMEM(tile, f32)],
        scal, qg, kv, kvp, kvpp,
    )
    near_stats = shift(stats, -1)
    far_stats = shift(stats[:8], -2)
    query_grad = flat(gather_back(dq))
    part = call(
        own_key_kernel,
        jax.ShapeDtypeStruct((SIDE, 2, HH, BLK, HD), f32),
        [pltpu.VMEM(tile, f32)],
        scal, qg, kv, stats,
    )
    dkv = call(
        far_key_kernel,
        jax.ShapeDtypeStruct((SIDE, 2, HH, BLK, HD), jnp.bfloat16),
        [pltpu.VMEM(tile, f32)],
        scal, qgn, qgnn, kv, near_stats, far_stats, part,
    )
    back = gather_back(dkv)
    return query_grad, flat(back[:, 0]), flat(back[:, 1])


def solution(mesh):
    cube = Mesh(np.asarray(mesh.devices).reshape(4, 2, 8, SIDE), SEQ + ("x",))
    rows = P(SEQ + ("x",), None)
    return jax.shard_map(
        per_device,
        mesh=cube,
        in_specs=(rows, rows, rows, rows, P()),
        out_specs=(rows, rows, rows),
        check_vma=False,
    )
```

time: 303 us -> 133 us (0.44)
  waiting for transfers between devices: 141 us -> 36.7 us
  starting transfers between devices: 114 us -> 50.9 us
  matrix products: 36.7 us -> 0 us
  Pallas kernels: 0 us -> 29.2 us
  other arithmetic: 0.53 us -> 4.74 us
    ppermute x35 -> x8, waiting for transfers between devices: 141 us -> 8.63 us  [shift(): return lax.ppermute(value, SEQ, pairs)]
    ppermute x35 -> x8, starting transfers between devices: 114 us -> 33.7 us  [shift(): return lax.ppermute(value, SEQ, pairs)]
    dot_general x41 -> x0, matrix products: 36.7 us -> none  [the longest x6 10.4 us: pair_grads(): jnp.einsum('hqk,qhd->khd', probs_low, out_grad, preferred_element_type=jn...]
    pallas_call x0 -> x3, Pallas kernels: none -> 29.2 us  [call(): pl.pallas_call(kernel, out_shape=outs, in_specs=specs, out_specs=jax.tree...]
    all_to_all x0 -> x4, waiting for transfers between devices: none -> 28 us  [the longest x2 18.4 us: spread(): return lax.all_to_all(jnp.transpose(both, (2, 0, 3, 1, 4)), 'x', 0, 0)]
    all_to_all x0 -> x4, starting transfers between devices: none -> 17.2 us  [the longest x2 9.27 us: gather_back(): mine = lax.all_to_all(blocks, 'x', 0, 0)]
  transfers between devices with their start and end apart: 35 -> 12, of which waited for: 19 -> 5; matrix products, arithmetic and copies ran while one was open for 13% -> 6% of each run, Pallas kernels for 0% -> 22%
where the time goes in v1:
time: 133 us; the launch traced here: 132 us
  starting transfers between devices  50.9 us (38%)
  waiting for transfers between devices  36.7 us (28%)
  Pallas kernels  29.2 us (22%)
  local copies, waits for them, and re-layouts  9.06 us (7%)
  other arithmetic  4.74 us (4%)
  between operations  1.53 us (1%)
    ppermute x8, starting transfers between devices, shift(): return lax.ppermute(value, SEQ, pairs)  33.7 us
    pallas_call x3, Pallas kernels, call(): pl.pallas_call(kernel, out_shape=outs, in_specs=specs, out_specs=jax.tree...  29.2 us
    all_to_all x2, waiting for transfers between devices, spread(): return lax.all_to_all(jnp.transpose(both, (2, 0, 3, 1, 4)), 'x', 0, 0)  18.4 us
    all_to_all x2, waiting for transfers between devices, gather_back(): mine = lax.all_to_all(blocks, 'x', 0, 0)  9.59 us
    all_to_all x2, starting transfers between devices, gather_back(): mine = lax.all_to_all(blocks, 'x', 0, 0)  9.27 us
    ppermute x8, waiting for transfers between devices, shift(): return lax.ppermute(value, SEQ, pairs)  8.63 us
    all_to_all x2, starting transfers between devices, spread(): return lax.all_to_all(jnp.transpose(both, (2, 0, 3, 1, 4)), 'x', 0, 0)  7.94 us
    unnamed x13, local copies, waits for them, and re-layouts  5.23 us
  transfers between devices with their start and end apart: 12, of which 5 were waited for; matrix products, arithmetic and copies ran while one was open for 6% of the time, Pallas kernels for 22%

profile of v1, /device:TPU:24, one launch (start us, length us, event | category | flops | bytes accessed | tf_op | source)
XLA Modules:
  0.0 132.1 jit_solution(4853838140350361927)
XLA Ops:
  0.6 1.4 %copy.12 = bf16[128,2048]{0,1:T(8,128)(2,1)S(1)} copy(bf16[128,2048]{1,0:T(8,128)(2,1)} %param.6) | data formatting | bytes 1048576 | tf_op args[1]
  2.9 1.1 maximum_bitcast_fusion.1
  4.0 4.4 %all-to-all-start.1 = ((bf16[4,2,4,128,128]{4,3,2,1,0:T(8,128)(2,1)}), bf16[4,2,4,128,128]{4,3,2,1,0:T(8,128)(2,1)S(1)}, u32[]{:S(2)}, u32[]{:S(2)}) async-start(bf16[4,2,4,128,128]{4,3,2,1,0:T(8,128)(2,1)} %maximum_bitcast_fusion.1), calls=%async_computation.1 | async-start | bytes 2097152 | tf_op jit(solution)/shard_map/all_to_all | solution.py:182
  9.5 1.1 maximum_bitcast_fusion
  10.6 12.9 %all-to-all-done.1.kv = bf16[4,2,4,128,128]{4,3,2,1,0:T(8,128)(2,1)S(1)} async-done(((bf16[4,2,4,128,128]{4,3,2,1,0:T(8,128)(2,1)}), bf16[4,2,4,128,128]{4,3,2,1,0:T(8,128)(2,1)S(1)}, u32[]{:S(2)}, u32[]{:S(2)}) %all-to-all-start.1) | async-done | bytes 1048608 | tf_op jit(solution)/shard_map/all_to_all | solution.py:182
  23.5 3.5 %all-to-all-start = ((bf16[4,2,4,128,128]{4,3,2,1,0:T(8,128)(2,1)}), bf16[4,2,4,128,128]{4,3,2,1,0:T(8,128)(2,1)S(1)}, u32[]{:S(2)}, u32[]{:S(2)}) async-start(bf16[4,2,4,128,128]{4,3,2,1,0:T(8,128)(2,1)} %maximum_bitcast_fusion), calls=%async_computation | async-start | bytes 2097152 | tf_op jit(solution)/shard_map/all_to_all | solution.py:182
  28.0 3.8 %collective-permute-start = (bf16[3,2,4,128,128]{4,3,2,1,0:T(8,128)(2,1)}, bf16[3,2,4,128,128]{4,3,2,1,0:T(8,128)(2,1)}, u32[]{:S(2)}, u32[]{:S(2)}) collective-permute-start(bf16[3,2,4,128,128]{4,3,2,1,0:T(8,128)(2,1)} %slice.28), channel_id=1, source_target_pairs={{0,4},{4,8},{8,12},{12,16},{16,20},{20,24},{24,28},{28,32},{32,36}... | collective-permute-start | bytes 2359304 | tf_op jit(solution)/shard_map/ppermute | solution.py:177
  31.8 3.8 %collective-permute-start.1 = (bf16[2,4,128,128]{3,2,1,0:T(8,128)(2,1)S(1)}, bf16[2,4,128,128]{3,2,1,0:T(8,128)(2,1)S(1)}, u32[]{:S(2)}, u32[]{:S(2)}) collective-permute-start(bf16[2,4,128,128]{3,2,1,0:T(8,128)(2,1)S(1)} %slice_bitcast_fusion.3), channel_id=1, source_target_pairs={{0,4},{4,8},{8,12},{12,16},{16,20},{20,24},{24,28},{28,32},{32,36}... | collective-permute-start | bytes 786440 | tf_op jit(solution)/shard_map/ppermute | solution.py:177
  35.6 5.6 %all-to-all-done.qg = bf16[4,2,4,128,128]{4,3,2,1,0:T(8,128)(2,1)S(1)} async-done(((bf16[4,2,4,128,128]{4,3,2,1,0:T(8,128)(2,1)}), bf16[4,2,4,128,128]{4,3,2,1,0:T(8,128)(2,1)S(1)}, u32[]{:S(2)}, u32[]{:S(2)}) %all-to-all-start) | async-done | bytes 1048608 | tf_op jit(solution)/shard_map/all_to_all | solution.py:182
  41.3 7.9 %collective-permute-start.4 = (bf16[3,2,4,128,128]{4,3,2,1,0:T(8,128)(2,1)S(1)}, bf16[3,2,4,128,128]{4,3,2,1,0:T(8,128)(2,1)}, u32[]{:S(2)}, u32[]{:S(2)}) collective-permute-start(bf16[3,2,4,128,128]{4,3,2,1,0:T(8,128)(2,1)S(1)} %slice.31), channel_id=1, source_target_pairs={{4,0},{8,4},{12,8},{16,12},{20,16},{24,20},{28,24},{32,28},{36,32}... | collective-permute-start | bytes 2359304 | tf_op jit(solution)/shard_map/ppermute | solution.py:177
  50.0 8.2 %collective-permute-done.1 = bf16[2,4,128,128]{3,2,1,0:T(8,128)(2,1)S(1)} collective-permute-done((bf16[2,4,128,128]{3,2,1,0:T(8,128)(2,1)S(1)}, bf16[2,4,128,128]{3,2,1,0:T(8,128)(2,1)S(1)}, u32[]{:S(2)}, u32[]{:S(2)}) %collective-permute-start.1) | collective-permute-done | bytes 262176 | tf_op jit(solution)/shard_map/ppermute | solution.py:177
  58.1 1.9 %collective-permute-start.2 = (bf16[2,4,128,128]{3,2,1,0:T(8,128)(2,1)S(1)}, bf16[2,4,128,128]{3,2,1,0:T(8,128)(2,1)S(1)}, u32[]{:S(2)}, u32[]{:S(2)}) collective-permute-start(bf16[2,4,128,128]{3,2,1,0:T(8,128)(2,1)S(1)} %collective-permute-done.1), channel_id=1, source_target_pairs={{0,4},{4,8},{8,12},{12,16},{16,20},{20,24},{24,28},{28,32},{32,36}... | collective-permute-start | bytes 786440 | tf_op jit(solution)/shard_map/ppermute | solution.py:177
  60.8 6.0 %collective-permute-start.3 = (bf16[2,4,128,128]{3,2,1,0:T(8,128)(2,1)}, bf16[2,4,128,128]{3,2,1,0:T(8,128)(2,1)}, u32[]{:S(2)}, u32[]{:S(2)}) collective-permute-start(bf16[2,4,128,128]{3,2,1,0:T(8,128)(2,1)} %slice_bitcast_fusion.2), channel_id=1, source_target_pairs={{4,0},{8,4},{12,8},{16,12},{20,16},{24,20},{28,24},{32,28},{36,32}... | collective-permute-start | bytes 786440 | tf_op jit(solution)/shard_map/ppermute | solution.py:177
  66.8 1.2 pad_maximum_fusion.kvp
  68.5 10.7 %shard_map.76 = (bf16[4,4,128,128]{3,2,1,0:T(8,128)(2,1)}, f32[32,128]{1,0:T(8,128)S(1)}) custom-call(s32[3]{0:T(128)S(1)} %pad_add_fusion.scal, bf16[4,2,4,128,128]{4,3,2,1,0:T(8,128)(2,1)S(1)} %all-to-all-done.qg, bf16[4,2,4,128,128]{4,3,2,1,0:T(8,128)(2,1)S(1)} %all-to-all-done.1.kv, bf16[4,2,4,128,128]{4,3,2,1,0:T(8,128)(2,1)S(1)} %pad_maximum_fusion.kvp, ...), custom_call_target="tpu_custom_call" | custom-call | tf_op jit(solution)/shard_map/pallas_call | solution.py:164
  79.2 4.5 %all-to-all-start.2 = ((bf16[4,4,128,128]{3,2,1,0:T(8,128)(2,1)}), bf16[4,4,128,128]{3,2,1,0:T(8,128)(2,1)S(1)}, u32[]{:S(2)}, u32[]{:S(2)}) async-start(bf16[4,4,128,128]{3,2,1,0:T(8,128)(2,1)} %get-tuple-element.5), calls=%async_computation.2 | async-start | bytes 1048576 | tf_op jit(solution)/shard_map/all_to_all | solution.py:186
  83.7 1.9 %collective-permute-start.5 = (bf16[2,4,128,128]{3,2,1,0:T(8,128)(2,1)}, bf16[2,4,128,128]{3,2,1,0:T(8,128)(2,1)S(1)}, u32[]{:S(2)}, u32[]{:S(2)}) collective-permute-start(bf16[2,4,128,128]{3,2,1,0:T(8,128)(2,1)} %collective-permute-done.3), channel_id=1, source_target_pairs={{4,0},{8,4},{12,8},{16,12},{20,16},{24,20},{28,24},{32,28},{36,32}... | collective-permute-start | bytes 786440 | tf_op jit(solution)/shard_map/ppermute | solution.py:177
  85.6 2.5 %collective-permute-start.6 = (f32[32,128]{1,0:T(8,128)S(1)}, f32[32,128]{1,0:T(8,128)S(1)}, u32[]{:S(2)}, u32[]{:S(2)}) collective-permute-start(f32[32,128]{1,0:T(8,128)S(1)} %get-tuple-element.6.stats), channel_id=1, source_target_pairs={{4,0},{8,4},{12,8},{16,12},{20,16},{24,20},{28,24},{32,28},{36,32}... | collective-permute-start | bytes 49160 | tf_op jit(solution)/shard_map/ppermute | solution.py:177
  88.2 5.8 %collective-permute-start.7 = (f32[8,128]{1,0:T(8,128)S(1)}, f32[8,128]{1,0:T(8,128)S(1)}, u32[]{:S(2)}, u32[]{:S(2)}) collective-permute-start(f32[8,128]{1,0:T(8,128)S(1)} %slice.25), channel_id=1, source_target_pairs={{8,0},{12,4},{16,8},{20,12},{24,16},{28,20},{32,24},{36,28},{40,32... | collective-permute-start | bytes 12296 | tf_op jit(solution)/shard_map/ppermute | solution.py:177
  93.9 1.3 pad_maximum_fusion.1.qgn
  95.2 6.7 %shard_map.77.part = f32[4,2,4,128,128]{4,3,2,1,0:T(8,128)S(1)} custom-call(s32[3]{0:T(128)S(1)} %pad_add_fusion.scal, bf16[4,2,4,128,128]{4,3,2,1,0:T(8,128)(2,1)S(1)} %all-to-all-done.qg, bf16[4,2,4,128,128]{4,3,2,1,0:T(8,128)(2,1)S(1)} %all-to-all-done.1.kv, f32[32,128]{1,0:T(8,128)S(1)} %get-tuple-element.6.stats), custom_call_target="tpu_custom_call" | custom-call | tf_op jit(solution)/shard_map/pallas_call | solution.py:164
  102.0 11.7 %shard_map.78 = bf16[4,2,4,128,128]{4,3,2,1,0:T(8,128)(2,1)} custom-call(s32[3]{0:T(128)S(1)} %pad_add_fusion.scal, bf16[4,2,4,128,128]{4,3,2,1,0:T(8,128)(2,1)S(1)} %pad_maximum_fusion.1.qgn, bf16[2,4,128,128]{3,2,1,0:T(8,128)(2,1)S(1)} %collective-permute-done.5.qgnn, bf16[4,2,4,128,128]{4,3,2,1,0:T(8,128)(2,1)S(1)} %all-to-all-done.1.kv, ...), custom_call_target="tpu_custom_call" | custom-call | tf_op jit(solution)/shard_map/pallas_call | solution.py:164
  113.7 4.8 %all-to-all-start.3 = ((bf16[4,2,4,128,128]{4,3,2,1,0:T(8,128)(2,1)}), bf16[4,2,4,128,128]{4,3,2,1,0:T(8,128)(2,1)S(1)}, u32[]{:S(2)}, u32[]{:S(2)}) async-start(bf16[4,2,4,128,128]{4,3,2,1,0:T(8,128)(2,1)} %shard_map.78), calls=%async_computation.3 | async-start | bytes 2097152 | tf_op jit(solution)/shard_map/all_to_all | solution.py:186
  119.8 9.6 %all-to-all-done.3 = bf16[4,2,4,128,128]{4,3,2,1,0:T(8,128)(2,1)S(1)} async-done(((bf16[4,2,4,128,128]{4,3,2,1,0:T(8,128)(2,1)}), bf16[4,2,4,128,128]{4,3,2,1,0:T(8,128)(2,1)S(1)}, u32[]{:S(2)}, u32[]{:S(2)}) %all-to-all-start.3) | async-done | bytes 1048608 | tf_op jit(solution)/shard_map/all_to_all | solution.py:186
  (34 shorter events, 8.2 us)
Async XLA Ops:
  0.6 1.7 %copy-start = (bf16[128,2048]{1,0:T(8,128)(2,1)S(1)}, bf16[128,2048]{1,0:T(8,128)(2,1)}, u32[]{:S(2)}) copy-start(bf16[128,2048]{1,0:T(8,128)(2,1)} %param.7) | copy-start | bytes 1572868
  2.9 5.5 %copy-start.1 = (bf16[128,2048]{1,0:T(8,128)(2,1)S(1)}, bf16[128,2048]{1,0:T(8,128)(2,1)}, u32[]{:S(2)}) copy-start(bf16[128,2048]{1,0:T(8,128)(2,1)} %param.5) | copy-start | bytes 1572868
  4.0 5.0 %copy-start.2 = (bf16[128,2048]{1,0:T(8,128)(2,1)S(1)}, bf16[128,2048]{1,0:T(8,128)(2,1)}, u32[]{:S(2)}) copy-start(bf16[128,2048]{1,0:T(8,128)(2,1)} %param.8) | copy-start | bytes 1572868
  4.0 19.5 %all-to-all-start.1 = ((bf16[4,2,4,128,128]{4,3,2,1,0:T(8,128)(2,1)}), bf16[4,2,4,128,128]{4,3,2,1,0:T(8,128)(2,1)S(1)}, u32[]{:S(2)}, u32[]{:S(2)}) async-start(bf16[4,2,4,128,128]{4,3,2,1,0:T(8,128)(2,1)} %maximum_bitcast_fusion.1), calls=%async_computation.1 | async-start | bytes 2097152 | tf_op jit(solution)/shard_map/all_to_all | solution.py:182
  23.5 17.7 %all-to-all-start = ((bf16[4,2,4,128,128]{4,3,2,1,0:T(8,128)(2,1)}), bf16[4,2,4,128,128]{4,3,2,1,0:T(8,128)(2,1)S(1)}, u32[]{:S(2)}, u32[]{:S(2)}) async-start(bf16[4,2,4,128,128]{4,3,2,1,0:T(8,128)(2,1)} %maximum_bitcast_fusion), calls=%async_computation | async-start | bytes 2097152 | tf_op jit(solution)/shard_map/all_to_all | solution.py:182
  28.0 38.8 %collective-permute-start = (bf16[3,2,4,128,128]{4,3,2,1,0:T(8,128)(2,1)}, bf16[3,2,4,128,128]{4,3,2,1,0:T(8,128)(2,1)}, u32[]{:S(2)}, u32[]{:S(2)}) collective-permute-start(bf16[3,2,4,128,128]{4,3,2,1,0:T(8,128)(2,1)} %slice.28), channel_id=1, source_target_pairs={{0,4},{4,8},{8,12},{12,16},{16,20},{20,24},{24,28},{28,32},{32,36}... | collective-permute-start | bytes 2359304 | tf_op jit(solution)/shard_map/ppermute | solution.py:177
  31.8 26.3 %collective-permute-start.1 = (bf16[2,4,128,128]{3,2,1,0:T(8,128)(2,1)S(1)}, bf16[2,4,128,128]{3,2,1,0:T(8,128)(2,1)S(1)}, u32[]{:S(2)}, u32[]{:S(2)}) collective-permute-start(bf16[2,4,128,128]{3,2,1,0:T(8,128)(2,1)S(1)} %slice_bitcast_fusion.3), channel_id=1, source_target_pairs={{0,4},{4,8},{8,12},{12,16},{16,20},{20,24},{24,28},{28,32},{32,36}... | collective-permute-start | bytes 786440 | tf_op jit(solution)/shard_map/ppermute | solution.py:177
  41.3 52.7 %collective-permute-start.4 = (bf16[3,2,4,128,128]{4,3,2,1,0:T(8,128)(2,1)S(1)}, bf16[3,2,4,128,128]{4,3,2,1,0:T(8,128)(2,1)}, u32[]{:S(2)}, u32[]{:S(2)}) collective-permute-start(bf16[3,2,4,128,128]{4,3,2,1,0:T(8,128)(2,1)S(1)} %slice.31), channel_id=1, source_target_pairs={{4,0},{8,4},{12,8},{16,12},{20,16},{24,20},{28,24},{32,28},{36,32}... | collective-permute-start | bytes 2359304 | tf_op jit(solution)/shard_map/ppermute | solution.py:177
  58.1 10.4 %collective-permute-start.2 = (bf16[2,4,128,128]{3,2,1,0:T(8,128)(2,1)S(1)}, bf16[2,4,128,128]{3,2,1,0:T(8,128)(2,1)S(1)}, u32[]{:S(2)}, u32[]{:S(2)}) collective-permute-start(bf16[2,4,128,128]{3,2,1,0:T(8,128)(2,1)S(1)} %collective-permute-done.1), channel_id=1, source_target_pairs={{0,4},{4,8},{8,12},{12,16},{16,20},{20,24},{24,28},{28,32},{32,36}... | collective-permute-start | bytes 786440 | tf_op jit(solution)/shard_map/ppermute | solution.py:177
  60.8 22.9 %collective-permute-start.3 = (bf16[2,4,128,128]{3,2,1,0:T(8,128)(2,1)}, bf16[2,4,128,128]{3,2,1,0:T(8,128)(2,1)}, u32[]{:S(2)}, u32[]{:S(2)}) collective-permute-start(bf16[2,4,128,128]{3,2,1,0:T(8,128)(2,1)} %slice_bitcast_fusion.2), channel_id=1, source_target_pairs={{4,0},{8,4},{12,8},{16,12},{20,16},{24,20},{28,24},{32,28},{36,32}... | collective-permute-start | bytes 786440 | tf_op jit(solution)/shard_map/ppermute | solution.py:177
  79.2 34.5 %all-to-all-start.2 = ((bf16[4,4,128,128]{3,2,1,0:T(8,128)(2,1)}), bf16[4,4,128,128]{3,2,1,0:T(8,128)(2,1)S(1)}, u32[]{:S(2)}, u32[]{:S(2)}) async-start(bf16[4,4,128,128]{3,2,1,0:T(8,128)(2,1)} %get-tuple-element.5), calls=%async_computation.2 | async-start | bytes 1048576 | tf_op jit(solution)/shard_map/all_to_all | solution.py:186
  83.7 18.3 %collective-permute-start.5 = (bf16[2,4,128,128]{3,2,1,0:T(8,128)(2,1)}, bf16[2,4,128,128]{3,2,1,0:T(8,128)(2,1)S(1)}, u32[]{:S(2)}, u32[]{:S(2)}) collective-permute-start(bf16[2,4,128,128]{3,2,1,0:T(8,128)(2,1)} %collective-permute-done.3), channel_id=1, source_target_pairs={{4,0},{8,4},{12,8},{16,12},{20,16},{24,20},{28,24},{32,28},{36,32}... | collective-permute-start | bytes 786440 | tf_op jit(solution)/shard_map/ppermute | solution.py:177
  85.6 16.4 %collective-permute-start.6 = (f32[32,128]{1,0:T(8,128)S(1)}, f32[32,128]{1,0:T(8,128)S(1)}, u32[]{:S(2)}, u32[]{:S(2)}) collective-permute-start(f32[32,128]{1,0:T(8,128)S(1)} %get-tuple-element.6.stats), channel_id=1, source_target_pairs={{4,0},{8,4},{12,8},{16,12},{20,16},{24,20},{28,24},{32,28},{36,32}... | collective-permute-start | bytes 49160 | tf_op jit(solution)/shard_map/ppermute | solution.py:177
  88.2 13.8 %collective-permute-start.7 = (f32[8,128]{1,0:T(8,128)S(1)}, f32[8,128]{1,0:T(8,128)S(1)}, u32[]{:S(2)}, u32[]{:S(2)}) collective-permute-start(f32[8,128]{1,0:T(8,128)S(1)} %slice.25), channel_id=1, source_target_pairs={{8,0},{12,4},{16,8},{20,12},{24,16},{28,20},{32,24},{36,28},{40,32... | collective-permute-start | bytes 12296 | tf_op jit(solution)/shard_map/ppermute | solution.py:177
  113.7 15.7 %all-to-all-start.3 = ((bf16[4,2,4,128,128]{4,3,2,1,0:T(8,128)(2,1)}), bf16[4,2,4,128,128]{4,3,2,1,0:T(8,128)(2,1)S(1)}, u32[]{:S(2)}, u32[]{:S(2)}) async-start(bf16[4,2,4,128,128]{4,3,2,1,0:T(8,128)(2,1)} %shard_map.78), calls=%async_computation.3 | async-start | bytes 2097152 | tf_op jit(solution)/shard_map/all_to_all | solution.py:186

commit v2 on v0

v2 whole, which is shorter than its diff:
```python
import math

import jax
import jax.numpy as jnp
import numpy as np
from jax import lax
from jax.experimental import pallas as pl
from jax.experimental.pallas import tpu as pltpu
from jax.sharding import Mesh
from jax.sharding import PartitionSpec as P


HEADS = 16
HD = 128
BLK = 128
SIDE = 4
HC = HEADS // SIDE
SCALE = HD ** (-0.5)
SCALE2 = SCALE * math.log2(math.e)
OFF = -1e30
GROUPS = ("o", "yl", "z")
INSIDE = "x"
BF = jnp.bfloat16
F32 = jnp.float32

NT = (((1,), (1,)), ((), ()))
NN = (((1,), (0,)), ((), ()))


def dot(a, b, dims):
    return lax.dot_general(a, b, dims, preferred_element_type=F32)


def mask_tile(width, blocks, shape, query_axis):
    query = lax.broadcasted_iota(jnp.int32, shape, query_axis)
    key = lax.broadcasted_iota(jnp.int32, shape, 1 - query_axis)
    back = query - key + blocks * BLK
    return jnp.where((back >= 0) & (back < width), 0.0, OFF).astype(F32)


def pack_kernel(first, second, out, sems):
    copies = []
    for dest in range(SIDE):
        for which, ref in enumerate((first, second)):
            for h in range(HC):
                lane = (dest * HC + h) * HD
                copies.append(
                    pltpu.make_async_copy(
                        ref.at[:, lane : lane + HD], out.at[dest, which, h], sems.at[len(copies)]
                    )
                )
    for copy in copies:
        copy.start()
    for copy in copies:
        copy.wait()


def unpack_kernel(back, *rest):
    outs, sems = rest[:-1], rest[-1]
    copies = []
    for which, out in enumerate(outs):
        for source in range(SIDE):
            for h in range(HC):
                lane = (source * HC + h) * HD
                copies.append(
                    pltpu.make_async_copy(
                        back.at[source, which, h], out.at[:, lane : lane + HD], sems.at[len(copies)]
                    )
                )
    for copy in copies:
        copy.start()
    for copy in copies:
        copy.wait()


def joined(blocks):
    return blocks[0] if len(blocks) == 1 else jnp.concatenate(blocks, axis=0)


A_TILES = (5, 4, 3, 0, -1)
A_STEPS = ((0, 1), (2, 3), (4, 5), (6,))


def fill_a(width, bias):
    for at, blocks in enumerate(A_TILES):
        bias[at] = mask_tile(width, blocks, (2 * BLK, BLK), 0)


def query_half(j, h, group, qg, keys, bias, wts, prods, cols):
    shape = (2 * BLK, BLK)
    query = joined([qg[j, 0, h], qg[j + 1, 0, h]])
    grad = joined([qg[j, 1, h], qg[j + 1, 1, h]])
    norm = jnp.zeros(shape, F32)
    centre = jnp.zeros(shape, F32)
    for steps in A_STEPS:
        logits2 = dot(query, joined([keys(j + s, 0, h) for s in steps]), NT)
        product2 = dot(grad, joined([keys(j + s, 1, h) for s in steps]), NT)
        for part, step in enumerate(steps):
            at, blocks = j + step, 5 - step
            logits = logits2[:, part * BLK : (part + 1) * BLK] * SCALE2
            product = product2[:, part * BLK : (part + 1) * BLK]
            if blocks in A_TILES:
                logits = logits + bias[A_TILES.index(blocks)]
            if at <= SIDE:
                behind = group > 0 if at else group > 1
                logits = logits + jnp.where(behind, 0.0, OFF).astype(F32)
            weight = jnp.exp2(logits)
            wts[step] = weight
            prods[step] = product
            norm = norm + weight
            centre = centre + weight * product
    norm = jnp.sum(norm, axis=1, keepdims=True)
    inverse = 1.0 / norm
    centre = jnp.sum(centre, axis=1, keepdims=True) * inverse
    total = jnp.zeros(shape, F32)
    for steps in A_STEPS:
        change = [(wts[s] * inverse) * (prods[s] - centre) for s in steps]
        change = change[0] if len(steps) == 1 else jnp.concatenate(change, axis=1)
        total = total + dot(change.astype(BF), joined([keys(j + s, 0, h) for s in steps]), NN)
    lane = lax.broadcasted_iota(jnp.int32, shape, 1)
    cols[...] = jnp.where(
        lane == h, jnp.log2(norm), jnp.where(lane == HC + h, centre, cols[...])
    )
    return (total * SCALE).astype(BF)


def rows_of(cols):
    rows = jnp.transpose(cols[...])[:8]
    return rows[:, :BLK], rows[:, BLK:]


def early_kernel(scal, qg, kv, kvp, dq, stats, part, cols, bias, bias_b, wts, prods):
    fill_a(scal[0], bias)
    fill_b(scal[0], bias_b)
    cols[...] = jnp.zeros_like(cols)

    def keys(at, which, h):
        return kvp[at - 1, which, h] if at <= SIDE else kv[at - SIDE - 1, which, h]

    def head(h, carry):
        total = query_half(2, h, scal[1], qg, keys, bias, wts, prods, cols)
        dq[0, 0, h] = total[:BLK]
        dq[1, 0, h] = total[BLK:]
        return carry

    lax.fori_loop(0, HC, head, 0)
    stats[:8], stats[8:] = rows_of(cols)

    def key_head(h, carry):
        for half, steps in ((0, (2, 3)), (1, (0, 1))):
            j = 2 * half
            zero = jnp.zeros((2 * BLK, HD), F32)
            dk, dv = key_half(
                [steps],
                joined([kv[j, 0, h], kv[j + 1, 0, h]]),
                joined([kv[j, 1, h], kv[j + 1, 1, h]]),
                lambda s, which: qg[j + s, which, h],
                lambda s: stats_rows(stats, j + s - 2, h),
                bias_b, zero, zero,
            )
            part[half, 0, h] = dk
            part[half, 1, h] = dv
        return carry

    lax.fori_loop(0, HC, key_head, 0)


def query_kernel(scal, qg, kv, kvp, kvpp, dq_late, stats_late, dq, stats, front, cols, bias, wts, prods):
    fill_a(scal[0], bias)
    cols[...] = jnp.zeros_like(cols)
    dq[2:] = dq_late[...]
    stats[16:] = stats_late[...]

    def keys(at, which, h):
        if at == 0:
            return kvpp[which, h]
        return kvp[at - 1, which, h] if at <= SIDE else kv[at - SIDE - 1, which, h]

    def head(h, carry):
        total = query_half(0, h, scal[1], qg, keys, bias, wts, prods, cols)
        dq[0, 0, h] = total[:BLK]
        dq[1, 0, h] = total[BLK:]
        return carry

    lax.fori_loop(0, HC, head, 0)
    first, second = rows_of(cols)
    front[...] = first
    stats[:8] = first
    stats[8:16] = second


def stats_rows(stats, block, h):
    return stats[pl.ds(block * 8 + h, 1)], stats[pl.ds(block * 8 + HC + h, 1)]


B_TILES = (0, 1, 4, 5, 6)


def fill_b(width, bias):
    for at, blocks in enumerate(B_TILES):
        bias[at] = mask_tile(width, blocks, (2 * BLK, BLK), 1)


def key_half(steps_of, key, value, queries, stats_of, bias, dk, dv):
    for steps in steps_of:
        query = joined([queries(s, 0) for s in steps])
        grad = joined([queries(s, 1) for s in steps])
        logits2 = dot(key, query, NT)
        product2 = dot(value, grad, NT)
        probs2, change2 = [], []
        for part, step in enumerate(steps):
            log_norm, centre = stats_of(step)
            logits = logits2[:, part * BLK : (part + 1) * BLK] * SCALE2 - log_norm
            if step in B_TILES:
                logits = logits + bias[B_TILES.index(step)]
            probs = jnp.exp2(logits)
            probs2.append(probs.astype(BF))
            change = probs * (product2[:, part * BLK : (part + 1) * BLK] - centre)
            change2.append(change.astype(BF))
        probs2 = probs2[0] if len(steps) == 1 else jnp.concatenate(probs2, axis=1)
        change2 = change2[0] if len(steps) == 1 else jnp.concatenate(change2, axis=1)
        dv = dv + dot(probs2, grad, NN)
        dk = dk + dot(change2, query, NN)
    return dk, dv


def far_key_kernel(
    scal, qg, qgn, qgnn, kv, stats, near, after, part_hbm, out, bias, part, sem
):
    fetch = pltpu.make_async_copy(part_hbm, part, sem)
    fetch.start()
    fill_b(scal[0], bias)

    def queries(at, which, h):
        if at < SIDE:
            return qg[at, which, h]
        return qgnn[which, h] if at == 2 * SIDE else qgn[at - SIDE, which, h]

    def stats_of(at, h):
        if at < SIDE:
            return stats_rows(stats, at, h)
        return stats_rows(after, 0, h) if at == 2 * SIDE else stats_rows(near, at - SIDE, h)

    fetch.wait()

    def head(h, carry):
        for half, todo in ((0, ((0, 1), (4, 5), (6,))), (1, ((2, 3), (4, 5), (6,)))):
            j = 2 * half
            dk, dv = key_half(
                todo,
                joined([kv[j, 0, h], kv[j + 1, 0, h]]),
                joined([kv[j, 1, h], kv[j + 1, 1, h]]),
                lambda s, which: queries(j + s, which, h),
                lambda s: stats_of(j + s, h),
                bias, part[half, 0, h], part[half, 1, h],
            )
            dk = (dk * SCALE).astype(BF)
            dv = dv.astype(BF)
            out[j, 0, h] = dk[:BLK]
            out[j + 1, 0, h] = dk[BLK:]
            out[j, 1, h] = dv[:BLK]
            out[j + 1, 1, h] = dv[BLK:]
        return carry

    lax.fori_loop(0, HC, head, 0)


VM = pl.BlockSpec(memory_space=pltpu.VMEM)
HBM = pl.BlockSpec(memory_space=pltpu.HBM)
PARAMS = pltpu.CompilerParams(vmem_limit_bytes=20 * 1024 * 1024)


def call(kernel, outs, scratch, scal, *args, specs=None):
    return pl.pallas_call(
        kernel,
        out_shape=outs,
        in_specs=[pl.BlockSpec(memory_space=pltpu.SMEM)] + (specs or [VM for _ in args]),
        out_specs=jax.tree.map(lambda _: VM, outs),
        scratch_shapes=scratch,
        compiler_params=PARAMS,
    )(scal, *args)


def in_hbm(value):
    return pltpu.with_memory_space_constraint(value, pltpu.HBM)


def blocks_of(arrays, blocks=SIDE):
    return jax.ShapeDtypeStruct((blocks, arrays, HC, BLK, HD), BF)


def pack(first, second):
    return pl.pallas_call(
        pack_kernel,
        out_shape=blocks_of(2),
        in_specs=[HBM, HBM],
        out_specs=VM,
        scratch_shapes=[pltpu.SemaphoreType.DMA((2 * HEADS,))],
        compiler_params=PARAMS,
    )(in_hbm(first), in_hbm(second))


def unpack(back):
    arrays = back.shape[1]
    rows = jax.ShapeDtypeStruct((BLK, HEADS * HD), BF)
    return pl.pallas_call(
        unpack_kernel,
        out_shape=[rows] * arrays,
        in_specs=[VM],
        out_specs=[HBM] * arrays,
        scratch_shapes=[pltpu.SemaphoreType.DMA((arrays * HEADS,))],
        compiler_params=PARAMS,
    )(back)


def shift(value, steps):
    count = lax.axis_size(GROUPS)
    pairs = [(at, at + steps) for at in range(count) if 0 <= at + steps < count]
    return lax.ppermute(value, GROUPS, pairs)


def swap(value):
    return lax.all_to_all(value, INSIDE, 0, 0)


def steps(queries, keys, values, grad_out, window):
    group = lax.axis_index(GROUPS)
    scal = jnp.stack([window[0], group]).astype(jnp.int32)
    packed = pack(keys, values)
    kv = swap(packed)
    packed = pack(queries, grad_out)
    raw = shift(packed, -1)
    kvp = shift(kv, 1)
    kvpp = shift(kv[SIDE - 1], 2)
    qg = swap(packed)
    qgnn = shift(qg[0], -2)
    qgn = swap(raw)
    tiles = pltpu.VMEM((5, 2 * BLK, BLK), F32)
    row_tiles = pltpu.VMEM((7, 2 * BLK, BLK), F32)
    cols = pltpu.VMEM((2 * BLK, BLK), F32)
    part_shape = (SIDE // 2, 2, HC, 2 * BLK, HD)
    dq_late, stats_late, part = call(
        early_kernel,
        [
            blocks_of(1, 2),
            jax.ShapeDtypeStruct((16, BLK), F32),
            jax.ShapeDtypeStruct(part_shape, F32),
        ],
        [cols, tiles, tiles, row_tiles, row_tiles],
        scal, qg, kv, kvp,
    )
    dq, stats, front = call(
        query_kernel,
        [
            blocks_of(1),
            jax.ShapeDtypeStruct((8 * SIDE, BLK), F32),
            jax.ShapeDtypeStruct((8, BLK), F32),
        ],
        [cols, tiles, row_tiles, row_tiles],
        scal, qg, kv, kvp, kvpp, dq_late, stats_late,
    )
    near = shift(stats, -1)
    after = shift(front, -2)
    back = swap(in_hbm(dq))
    (query_grad,) = unpack(back)
    dkv = call(
        far_key_kernel, blocks_of(2),
        [tiles, pltpu.VMEM(part_shape, F32), pltpu.SemaphoreType.DMA(())],
        scal, qg, qgn, qgnn, kv, stats, near, after, in_hbm(part),
        specs=[VM] * 7 + [HBM],
    )
    back = swap(dkv)
    key_grad, value_grad = unpack(back)
    return query_grad, key_grad, value_grad


def solution(mesh):
    cube = Mesh(np.asarray(mesh.devices).reshape(4, 2, 8, SIDE), GROUPS + ("x",))
    rows = P(GROUPS + ("x",), None)
    return jax.shard_map(
        steps,
        mesh=cube,
        in_specs=(rows, rows, rows, rows, P()),
        out_specs=(rows, rows, rows),
        check_vma=False,
    )
```

time: 303 us -> 125 us (0.41)
  the two profiles are of different devices: /device:TPU:24 before, /device:TPU:1 now
where the time goes in v2:
time: 125 us
  starting transfers between devices  56.4 us (45%)
  waiting for transfers between devices  35.8 us (29%)
  Pallas kernels  26.9 us (22%)
  local copies, waits for them, and re-layouts  3.85 us (3%)
  between operations  1.42 us (1%)
    ppermute x6, starting transfers between devices, shift(): return lax.ppermute(value, GROUPS, pairs)  35.6 us
    all_to_all x5, waiting for transfers between devices, swap(): return lax.all_to_all(value, INSIDE, 0, 0)  21.5 us
    all_to_all x5, starting transfers between devices, swap(): return lax.all_to_all(value, INSIDE, 0, 0)  20.8 us
    pallas_call x3, Pallas kernels, call(): pl.pallas_call(kernel, out_shape=outs, in_specs=[pl.BlockSpec(memory_spac...  18.8 us
    ppermute x6, waiting for transfers between devices, shift(): return lax.ppermute(value, GROUPS, pairs)  14.4 us
    pallas_call x2, Pallas kernels, pack(): pl.pallas_call(pack_kernel, out_shape=blocks_of(2), in_specs=[HBM, HBM],...  4.9 us
    pallas_call x2, Pallas kernels, unpack(): pl.pallas_call(unpack_kernel, out_shape=[rows] * arrays, in_specs=[VM], o...  3.18 us
    unnamed x6, local copies, waits for them, and re-layouts  3.12 us
  transfers between devices with their start and end apart: 11, of which 7 were waited for; matrix products, arithmetic and copies ran while one was open for 1% of the time, Pallas kernels for 19%

profile of v2, /device:TPU:1, one launch (start us, length us, event | category | flops | bytes accessed | tf_op | source)
XLA Modules:
  0.0 124.5 jit_solution(9720888061922770258)
XLA Ops:
  0.6 2.4 %shard_map.77 = bf16[4,2,4,128,128]{4,3,2,1,0:T(8,128)(2,1)} custom-call(bf16[128,2048]{1,0:T(8,128)(2,1)} %first.3, bf16[128,2048]{1,0:T(8,128)(2,1)} %second.3), custom_call_target="tpu_custom_call" | custom-call | tf_op jit(solution)/shard_map/pallas_call | solution.py:293
  3.1 4.8 %all-to-all-start.1 = ((bf16[4,2,4,128,128]{4,3,2,1,0:T(8,128)(2,1)}), bf16[4,2,4,128,128]{4,3,2,1,0:T(8,128)(2,1)S(1)}, u32[]{:S(2)}, u32[]{:S(2)}) async-start(bf16[4,2,4,128,128]{4,3,2,1,0:T(8,128)(2,1)} %shard_map.77), calls=%async_computation.1 | async-start | bytes 2097152 | tf_op jit(solution)/shard_map/all_to_all | solution.py:323
  7.9 2.5 %shard_map.76 = bf16[4,2,4,128,128]{4,3,2,1,0:T(8,128)(2,1)} custom-call(bf16[128,2048]{1,0:T(8,128)(2,1)} %first.2, bf16[128,2048]{1,0:T(8,128)(2,1)} %second.2), custom_call_target="tpu_custom_call" | custom-call | tf_op jit(solution)/shard_map/pallas_call | solution.py:293
  10.4 9.3 %collective-permute-start.2 = (bf16[4,2,4,128,128]{4,3,2,1,0:T(8,128)(2,1)}, bf16[4,2,4,128,128]{4,3,2,1,0:T(8,128)(2,1)}, u32[]{:S(2)}, u32[]{:S(2)}) collective-permute-start(bf16[4,2,4,128,128]{4,3,2,1,0:T(8,128)(2,1)} %shard_map.76), channel_id=1, source_target_pairs={{4,0},{8,4},{12,8},{16,12},{20,16},{24,20},{28,24},{32,28},{36,32}... | collective-permute-start | bytes 3145736 | tf_op jit(solution)/shard_map/ppermute | solution.py:319
  19.7 1.5 %all-to-all-done.1.kv = bf16[4,2,4,128,128]{4,3,2,1,0:T(8,128)(2,1)S(1)} async-done(((bf16[4,2,4,128,128]{4,3,2,1,0:T(8,128)(2,1)}), bf16[4,2,4,128,128]{4,3,2,1,0:T(8,128)(2,1)S(1)}, u32[]{:S(2)}, u32[]{:S(2)}) %all-to-all-start.1) | async-done | bytes 1048608 | tf_op jit(solution)/shard_map/all_to_all | solution.py:323
  21.3 3.5 %all-to-all-start = ((bf16[4,2,4,128,128]{4,3,2,1,0:T(8,128)(2,1)}), bf16[4,2,4,128,128]{4,3,2,1,0:T(8,128)(2,1)S(1)}, u32[]{:S(2)}, u32[]{:S(2)}) async-start(bf16[4,2,4,128,128]{4,3,2,1,0:T(8,128)(2,1)} %shard_map.76), calls=%async_computation | async-start | bytes 2097152 | tf_op jit(solution)/shard_map/all_to_all | solution.py:323
  24.8 4.5 %collective-permute-start = (bf16[4,2,4,128,128]{4,3,2,1,0:T(8,128)(2,1)S(1)}, bf16[4,2,4,128,128]{4,3,2,1,0:T(8,128)(2,1)}, u32[]{:S(2)}, u32[]{:S(2)}) collective-permute-start(bf16[4,2,4,128,128]{4,3,2,1,0:T(8,128)(2,1)S(1)} %all-to-all-done.1.kv), channel_id=1, source_target_pairs={{0,4},{4,8},{8,12},{12,16},{16,20},{20,24},{24,28},{28,32},{32,36}... | collective-permute-start | bytes 3145736 | tf_op jit(solution)/shard_map/ppermute | solution.py:319
  29.2 7.7 %all-to-all-done.qg = bf16[4,2,4,128,128]{4,3,2,1,0:T(8,128)(2,1)S(1)} async-done(((bf16[4,2,4,128,128]{4,3,2,1,0:T(8,128)(2,1)}), bf16[4,2,4,128,128]{4,3,2,1,0:T(8,128)(2,1)S(1)}, u32[]{:S(2)}, u32[]{:S(2)}) %all-to-all-start) | async-done | bytes 1048608 | tf_op jit(solution)/shard_map/all_to_all | solution.py:323
  36.9 3.5 %all-to-all-start.3 = ((bf16[4,2,4,128,128]{4,3,2,1,0:T(8,128)(2,1)}), bf16[4,2,4,128,128]{4,3,2,1,0:T(8,128)(2,1)S(1)}, u32[]{:S(2)}, u32[]{:S(2)}) async-start(bf16[4,2,4,128,128]{4,3,2,1,0:T(8,128)(2,1)} %collective-permute-done.2), calls=%async_computation.3 | async-start | bytes 2097152 | tf_op jit(solution)/shard_map/all_to_all | solution.py:323
  41.2 7.0 %collective-permute-start.1 = (bf16[2,4,128,128]{3,2,1,0:T(8,128)(2,1)}, bf16[2,4,128,128]{3,2,1,0:T(8,128)(2,1)S(1)}, u32[]{:S(2)}, u32[]{:S(2)}) collective-permute-start(bf16[2,4,128,128]{3,2,1,0:T(8,128)(2,1)} %slice_bitcast_fusion.1), channel_id=1, source_target_pairs={{0,8},{4,12},{8,16},{12,20},{16,24},{20,28},{24,32},{28,36},{32,40... | collective-permute-start | bytes 786440 | tf_op jit(solution)/shard_map/ppermute | solution.py:319
  48.9 12.4 %collective-permute-done.kvp = bf16[4,2,4,128,128]{4,3,2,1,0:T(8,128)(2,1)} collective-permute-done((bf16[4,2,4,128,128]{4,3,2,1,0:T(8,128)(2,1)S(1)}, bf16[4,2,4,128,128]{4,3,2,1,0:T(8,128)(2,1)}, u32[]{:S(2)}, u32[]{:S(2)}) %collective-permute-start) | collective-permute-done | bytes 1048608 | tf_op jit(solution)/shard_map/ppermute | solution.py:319
  61.3 6.8 %shard_map.78 = (bf16[2,1,4,128,128]{4,3,2,1,0:T(8,128)(2,1)S(1)}, f32[16,128]{1,0:T(8,128)S(1)}, f32[2,2,4,256,128]{4,3,2,1,0:T(8,128)S(1)}) custom-call(s32[2]{0:T(128)S(1)} %pad_add_fusion.scal, bf16[4,2,4,128,128]{4,3,2,1,0:T(8,128)(2,1)S(1)} %all-to-all-done.qg, bf16[4,2,4,128,128]{4,3,2,1,0:T(8,128)(2,1)S(1)} %all-to-all-done.1.kv, ...), custom_call_target="tpu_custom_call" | custom-call | tf_op jit(solution)/shard_map/pallas_call | solution.py:274
  68.1 1.3 %copy-done.1 = f32[2,2,4,256,128]{4,3,2,1,0:T(8,128)} copy-done((f32[2,2,4,256,128]{4,3,2,1,0:T(8,128)}, f32[2,2,4,256,128]{4,3,2,1,0:T(8,128)S(1)}, u32[]{:S(2)}) %copy-start.1) | copy-done | bytes 2097176
  69.4 4.4 %shard_map.79 = (bf16[4,1,4,128,128]{4,3,2,1,0:T(8,128)(2,1)S(1)}, f32[32,128]{1,0:T(8,128)S(1)}, f32[8,128]{1,0:T(8,128)S(1)}) custom-call(s32[2]{0:T(128)S(1)} %pad_add_fusion.scal, bf16[4,2,4,128,128]{4,3,2,1,0:T(8,128)(2,1)S(1)} %all-to-all-done.qg, bf16[4,2,4,128,128]{4,3,2,1,0:T(8,128)(2,1)S(1)} %all-to-all-done.1.kv, ...), custom_call_target="tpu_custom_call" | custom-call | tf_op jit(solution)/shard_map/pallas_call | solution.py:274
  74.6 4.7 %all-to-all-start.2 = ((bf16[4,1,4,128,128]{4,3,2,1,0:T(8,128)(2,1)}), bf16[4,1,4,128,128]{4,3,2,1,0:T(8,128)(2,1)}, u32[]{:S(2)}, u32[]{:S(2)}) async-start(bf16[4,1,4,128,128]{4,3,2,1,0:T(8,128)(2,1)} %copy-done.2), calls=%async_computation.2 | async-start | bytes 1048576 | tf_op jit(solution)/shard_map/all_to_all | solution.py:323
  79.4 8.7 %collective-permute-start.3 = (bf16[2,4,128,128]{3,2,1,0:T(8,128)(2,1)S(1)}, bf16[2,4,128,128]{3,2,1,0:T(8,128)(2,1)S(1)}, u32[]{:S(2)}, u32[]{:S(2)}) collective-permute-start(bf16[2,4,128,128]{3,2,1,0:T(8,128)(2,1)S(1)} %slice_bitcast_fusion), channel_id=1, source_target_pairs={{8,0},{12,4},{16,8},{20,12},{24,16},{28,20},{32,24},{36,28},{40,32... | collective-permute-start | bytes 786440 | tf_op jit(solution)/shard_map/ppermute | solution.py:319
  88.1 1.9 %collective-permute-start.4 = (f32[32,128]{1,0:T(8,128)S(1)}, f32[32,128]{1,0:T(8,128)S(1)}, u32[]{:S(2)}, u32[]{:S(2)}) collective-permute-start(f32[32,128]{1,0:T(8,128)S(1)} %get-tuple-element.14.stats), channel_id=1, source_target_pairs={{4,0},{8,4},{12,8},{16,12},{20,16},{24,20},{28,24},{32,28},{36,32}... | collective-permute-start | bytes 49160 | tf_op jit(solution)/shard_map/ppermute | solution.py:319
  90.0 4.2 %collective-permute-start.5 = (f32[8,128]{1,0:T(8,128)S(1)}, f32[8,128]{1,0:T(8,128)S(1)}, u32[]{:S(2)}, u32[]{:S(2)}) collective-permute-start(f32[8,128]{1,0:T(8,128)S(1)} %get-tuple-element.15), channel_id=1, source_target_pairs={{8,0},{12,4},{16,8},{20,12},{24,16},{28,20},{32,24},{36,28},{40,32... | collective-permute-start | bytes 12296 | tf_op jit(solution)/shard_map/ppermute | solution.py:319
  94.2 1.8 %collective-permute-done.3.qgnn = bf16[2,4,128,128]{3,2,1,0:T(8,128)(2,1)S(1)} collective-permute-done((bf16[2,4,128,128]{3,2,1,0:T(8,128)(2,1)S(1)}, bf16[2,4,128,128]{3,2,1,0:T(8,128)(2,1)S(1)}, u32[]{:S(2)}, u32[]{:S(2)}) %collective-permute-start.3) | collective-permute-done | bytes 262176 | tf_op jit(solution)/shard_map/ppermute | solution.py:319
  96.2 7.7 %shard_map.81 = bf16[4,2,4,128,128]{4,3,2,1,0:T(8,128)(2,1)S(1)} custom-call(s32[2]{0:T(128)S(1)} %pad_add_fusion.scal, bf16[4,2,4,128,128]{4,3,2,1,0:T(8,128)(2,1)S(1)} %all-to-all-done.qg, bf16[4,2,4,128,128]{4,3,2,1,0:T(8,128)(2,1)S(1)} %all-to-all-done.3.qgn, bf16[2,4,128,128]{3,2,1,0:T(8,128)(2,1)S(1)} %collective-permute-done.3.qgnn, ...), custom_call_target="tpu_custom_call" | custom-call | tf_op jit(solution)/shard_map/pallas_call | solution.py:274
  104.9 4.2 %all-to-all-start.4 = ((bf16[4,2,4,128,128]{4,3,2,1,0:T(8,128)(2,1)}), bf16[4,2,4,128,128]{4,3,2,1,0:T(8,128)(2,1)S(1)}, u32[]{:S(2)}, u32[]{:S(2)}) async-start(bf16[4,2,4,128,128]{4,3,2,1,0:T(8,128)(2,1)} %copy-done), calls=%async_computation.4 | async-start | bytes 2097152 | tf_op jit(solution)/shard_map/all_to_all | solution.py:323
  109.1 2.0 %shard_map.80 = bf16[128,2048]{1,0:T(8,128)(2,1)} custom-call(bf16[4,1,4,128,128]{4,3,2,1,0:T(8,128)(2,1)} %all-to-all-done.2.back), custom_call_target="tpu_custom_call" | custom-call | tf_op jit(solution)/shard_map/pallas_call | solution.py:306
  111.1 12.2 %all-to-all-done.4.back = bf16[4,2,4,128,128]{4,3,2,1,0:T(8,128)(2,1)S(1)} async-done(((bf16[4,2,4,128,128]{4,3,2,1,0:T(8,128)(2,1)}), bf16[4,2,4,128,128]{4,3,2,1,0:T(8,128)(2,1)S(1)}, u32[]{:S(2)}, u32[]{:S(2)}) %all-to-all-start.4) | async-done | bytes 1048608 | tf_op jit(solution)/shard_map/all_to_all | solution.py:323
  123.3 1.2 shard_map.82
  (14 shorter events, 2.8 us)
Async XLA Ops:
  3.1 18.2 %all-to-all-start.1 = ((bf16[4,2,4,128,128]{4,3,2,1,0:T(8,128)(2,1)}), bf16[4,2,4,128,128]{4,3,2,1,0:T(8,128)(2,1)S(1)}, u32[]{:S(2)}, u32[]{:S(2)}) async-start(bf16[4,2,4,128,128]{4,3,2,1,0:T(8,128)(2,1)} %shard_map.77), calls=%async_computation.1 | async-start | bytes 2097152 | tf_op jit(solution)/shard_map/all_to_all | solution.py:323
  10.4 26.5 %collective-permute-start.2 = (bf16[4,2,4,128,128]{4,3,2,1,0:T(8,128)(2,1)}, bf16[4,2,4,128,128]{4,3,2,1,0:T(8,128)(2,1)}, u32[]{:S(2)}, u32[]{:S(2)}) collective-permute-start(bf16[4,2,4,128,128]{4,3,2,1,0:T(8,128)(2,1)} %shard_map.76), channel_id=1, source_target_pairs={{4,0},{8,4},{12,8},{16,12},{20,16},{24,20},{28,24},{32,28},{36,32}... | collective-permute-start | bytes 3145736 | tf_op jit(solution)/shard_map/ppermute | solution.py:319
  21.3 15.7 %all-to-all-start = ((bf16[4,2,4,128,128]{4,3,2,1,0:T(8,128)(2,1)}), bf16[4,2,4,128,128]{4,3,2,1,0:T(8,128)(2,1)S(1)}, u32[]{:S(2)}, u32[]{:S(2)}) async-start(bf16[4,2,4,128,128]{4,3,2,1,0:T(8,128)(2,1)} %shard_map.76), calls=%async_computation | async-start | bytes 2097152 | tf_op jit(solution)/shard_map/all_to_all | solution.py:323
  24.8 36.5 %collective-permute-start = (bf16[4,2,4,128,128]{4,3,2,1,0:T(8,128)(2,1)S(1)}, bf16[4,2,4,128,128]{4,3,2,1,0:T(8,128)(2,1)}, u32[]{:S(2)}, u32[]{:S(2)}) collective-permute-start(bf16[4,2,4,128,128]{4,3,2,1,0:T(8,128)(2,1)S(1)} %all-to-all-done.1.kv), channel_id=1, source_target_pairs={{0,4},{4,8},{8,12},{12,16},{16,20},{20,24},{24,28},{28,32},{32,36}... | collective-permute-start | bytes 3145736 | tf_op jit(solution)/shard_map/ppermute | solution.py:319
  36.9 37.7 %all-to-all-start.3 = ((bf16[4,2,4,128,128]{4,3,2,1,0:T(8,128)(2,1)}), bf16[4,2,4,128,128]{4,3,2,1,0:T(8,128)(2,1)S(1)}, u32[]{:S(2)}, u32[]{:S(2)}) async-start(bf16[4,2,4,128,128]{4,3,2,1,0:T(8,128)(2,1)} %collective-permute-done.2), calls=%async_computation.3 | async-start | bytes 2097152 | tf_op jit(solution)/shard_map/all_to_all | solution.py:323
  41.2 28.2 %collective-permute-start.1 = (bf16[2,4,128,128]{3,2,1,0:T(8,128)(2,1)}, bf16[2,4,128,128]{3,2,1,0:T(8,128)(2,1)S(1)}, u32[]{:S(2)}, u32[]{:S(2)}) collective-permute-start(bf16[2,4,128,128]{3,2,1,0:T(8,128)(2,1)} %slice_bitcast_fusion.1), channel_id=1, source_target_pairs={{0,8},{4,12},{8,16},{12,20},{16,24},{20,28},{24,32},{28,36},{32,40... | collective-permute-start | bytes 786440 | tf_op jit(solution)/shard_map/ppermute | solution.py:319
  68.1 1.3 %copy-start.1 = (f32[2,2,4,256,128]{4,3,2,1,0:T(8,128)}, f32[2,2,4,256,128]{4,3,2,1,0:T(8,128)S(1)}, u32[]{:S(2)}) copy-start(f32[2,2,4,256,128]{4,3,2,1,0:T(8,128)S(1)} %get-tuple-element.16.part_hbm) | copy-start | bytes 6291460
  73.8 0.8 copy-start.2
  74.6 30.3 %all-to-all-start.2 = ((bf16[4,1,4,128,128]{4,3,2,1,0:T(8,128)(2,1)}), bf16[4,1,4,128,128]{4,3,2,1,0:T(8,128)(2,1)}, u32[]{:S(2)}, u32[]{:S(2)}) async-start(bf16[4,1,4,128,128]{4,3,2,1,0:T(8,128)(2,1)} %copy-done.2), calls=%async_computation.2 | async-start | bytes 1048576 | tf_op jit(solution)/shard_map/all_to_all | solution.py:323
  79.4 16.6 %collective-permute-start.3 = (bf16[2,4,128,128]{3,2,1,0:T(8,128)(2,1)S(1)}, bf16[2,4,128,128]{3,2,1,0:T(8,128)(2,1)S(1)}, u32[]{:S(2)}, u32[]{:S(2)}) collective-permute-start(bf16[2,4,128,128]{3,2,1,0:T(8,128)(2,1)S(1)} %slice_bitcast_fusion), channel_id=1, source_target_pairs={{8,0},{12,4},{16,8},{20,12},{24,16},{28,20},{32,24},{36,28},{40,32... | collective-permute-start | bytes 786440 | tf_op jit(solution)/shard_map/ppermute | solution.py:319
  88.1 8.1 %collective-permute-start.4 = (f32[32,128]{1,0:T(8,128)S(1)}, f32[32,128]{1,0:T(8,128)S(1)}, u32[]{:S(2)}, u32[]{:S(2)}) collective-permute-start(f32[32,128]{1,0:T(8,128)S(1)} %get-tuple-element.14.stats), channel_id=1, source_target_pairs={{4,0},{8,4},{12,8},{16,12},{20,16},{24,20},{28,24},{32,28},{36,32}... | collective-permute-start | bytes 49160 | tf_op jit(solution)/shard_map/ppermute | solution.py:319
  90.0 6.2 %collective-permute-start.5 = (f32[8,128]{1,0:T(8,128)S(1)}, f32[8,128]{1,0:T(8,128)S(1)}, u32[]{:S(2)}, u32[]{:S(2)}) collective-permute-start(f32[8,128]{1,0:T(8,128)S(1)} %get-tuple-element.15), channel_id=1, source_target_pairs={{8,0},{12,4},{16,8},{20,12},{24,16},{28,20},{32,24},{36,28},{40,32... | collective-permute-start | bytes 12296 | tf_op jit(solution)/shard_map/ppermute | solution.py:319
  103.9 1.0 copy-start
  104.9 18.4 %all-to-all-start.4 = ((bf16[4,2,4,128,128]{4,3,2,1,0:T(8,128)(2,1)}), bf16[4,2,4,128,128]{4,3,2,1,0:T(8,128)(2,1)S(1)}, u32[]{:S(2)}, u32[]{:S(2)}) async-start(bf16[4,2,4,128,128]{4,3,2,1,0:T(8,128)(2,1)} %copy-done), calls=%async_computation.4 | async-start | bytes 2097152 | tf_op jit(solution)/shard_map/all_to_all | solution.py:323

commit v3 on v2

--- a/solution.py
+++ b/solution.py
@@ -105,8 +105,8 @@
                 behind = group > 0 if at else group > 1
                 logits = logits + jnp.where(behind, 0.0, OFF).astype(F32)
             weight = jnp.exp2(logits)
-            wts[step] = weight
-            prods[step] = product
+            wts[h % 2, step] = weight
+            prods[h % 2, step] = product
             norm = norm + weight
             centre = centre + weight * product
     norm = jnp.sum(norm, axis=1, keepdims=True)
@@ -114,7 +114,7 @@
     centre = jnp.sum(centre, axis=1, keepdims=True) * inverse
     total = jnp.zeros(shape, F32)
     for steps in A_STEPS:
-        change = [(wts[s] * inverse) * (prods[s] - centre) for s in steps]
+        change = [(wts[h % 2, s] * inverse) * (prods[h % 2, s] - centre) for s in steps]
         change = change[0] if len(steps) == 1 else jnp.concatenate(change, axis=1)
         total = total + dot(change.astype(BF), joined([keys(j + s, 0, h) for s in steps]), NN)
     lane = lax.broadcasted_iota(jnp.int32, shape, 1)
@@ -129,7 +129,28 @@
     return rows[:, :BLK], rows[:, BLK:]
 
 
-def early_kernel(scal, qg, kv, kvp, dq, stats, part, cols, bias, bias_b, wts, prods):
+def head_copy(source, target, sems, h):
+    return pltpu.make_async_copy(source.at[:, :, h], target.at[:, :, h], sems.at[h])
+
+
+def finish_heads(source, target, sems):
+    for h in range(HC):
+        head_copy(source, target, sems, h).wait()
+
+
+def fetch_heads(source, target, sems):
+    def copy(h):
+        return head_copy(source, target, sems, h)
+
+    for h in range(HC):
+        copy(h).start()
+    return lambda h: copy(h).wait()
+
+
+def early_kernel(
+    scal, qg, kv, kvp_hbm, dq, stats, part_hbm, cols, bias, bias_b, wts, prods, kvp, part, sems, sems_out
+):
+    arrived = fetch_heads(kvp_hbm, kvp, sems)
     fill_a(scal[0], bias)
     fill_b(scal[0], bias_b)
     cols[...] = jnp.zeros_like(cols)
@@ -137,16 +158,17 @@
     def keys(at, which, h):
         return kvp[at - 1, which, h] if at <= SIDE else kv[at - SIDE - 1, which, h]
 
-    def head(h, carry):
+    def head(h):
+        arrived(h)
         total = query_half(2, h, scal[1], qg, keys, bias, wts, prods, cols)
         dq[0, 0, h] = total[:BLK]
         dq[1, 0, h] = total[BLK:]
-        return carry
-
-    lax.fori_loop(0, HC, head, 0)
+
+    for h in range(HC):
+        head(h)
     stats[:8], stats[8:] = rows_of(cols)
 
-    def key_head(h, carry):
+    def key_head(h):
         for half, steps in ((0, (2, 3)), (1, (0, 1))):
             j = 2 * half
             zero = jnp.zeros((2 * BLK, HD), F32)
@@ -160,15 +182,21 @@
             )
             part[half, 0, h] = dk
             part[half, 1, h] = dv
-        return carry
-
-    lax.fori_loop(0, HC, key_head, 0)
-
-
-def query_kernel(scal, qg, kv, kvp, kvpp, dq_late, stats_late, dq, stats, front, cols, bias, wts, prods):
+        head_copy(part, part_hbm, sems_out, h).start()
+
+    for h in range(HC):
+        key_head(h)
+    finish_heads(part, part_hbm, sems_out)
+
+
+def query_kernel(
+    scal, qg, kv, kvp_hbm, kvpp, dq_late, stats_late, dq_hbm, stats, front,
+    cols, bias, wts, prods, kvp, dq_own, sems, sems_out,
+):
+    arrived = fetch_heads(kvp_hbm, kvp, sems)
     fill_a(scal[0], bias)
     cols[...] = jnp.zeros_like(cols)
-    dq[2:] = dq_late[...]
+    dq_own[2:] = dq_late[...]
     stats[16:] = stats_late[...]
 
     def keys(at, which, h):
@@ -176,21 +204,24 @@
             return kvpp[which, h]
         return kvp[at - 1, which, h] if at <= SIDE else kv[at - SIDE - 1, which, h]
 
-    def head(h, carry):
+    def head(h):
+        arrived(h)
         total = query_half(0, h, scal[1], qg, keys, bias, wts, prods, cols)
-        dq[0, 0, h] = total[:BLK]
-        dq[1, 0, h] = total[BLK:]
-        return carry
-
-    lax.fori_loop(0, HC, head, 0)
+        dq_own[0, 0, h] = total[:BLK]
+        dq_own[1, 0, h] = total[BLK:]
+        head_copy(dq_own, dq_hbm, sems_out, h).start()
+
+    for h in range(HC):
+        head(h)
     first, second = rows_of(cols)
     front[...] = first
     stats[:8] = first
     stats[8:16] = second
+    finish_heads(dq_own, dq_hbm, sems_out)
 
 
 def stats_rows(stats, block, h):
-    return stats[pl.ds(block * 8 + h, 1)], stats[pl.ds(block * 8 + HC + h, 1)]
+    return stats[block * 8 + h : block * 8 + h + 1], stats[block * 8 + HC + h : block * 8 + HC + h + 1]
 
 
 B_TILES = (0, 1, 4, 5, 6)
@@ -225,10 +256,9 @@
 
 
 def far_key_kernel(
-    scal, qg, qgn, qgnn, kv, stats, near, after, part_hbm, out, bias, part, sem
+    scal, qg, qgn, qgnn, kv, stats, near, after, part_hbm, out_hbm, bias, part, out, sem, sems_out
 ):
-    fetch = pltpu.make_async_copy(part_hbm, part, sem)
-    fetch.start()
+    arrived = fetch_heads(part_hbm, part, sem)
     fill_b(scal[0], bias)
 
     def queries(at, which, h):
@@ -241,9 +271,8 @@
             return stats_rows(stats, at, h)
         return stats_rows(after, 0, h) if at == 2 * SIDE else stats_rows(near, at - SIDE, h)
 
-    fetch.wait()
-
-    def head(h, carry):
+    def head(h):
+        arrived(h)
         for half, todo in ((0, ((0, 1), (4, 5), (6,))), (1, ((2, 3), (4, 5), (6,)))):
             j = 2 * half
             dk, dv = key_half(
@@ -260,22 +289,26 @@
             out[j + 1, 0, h] = dk[BLK:]
             out[j, 1, h] = dv[:BLK]
             out[j + 1, 1, h] = dv[BLK:]
-        return carry
-
-    lax.fori_loop(0, HC, head, 0)
+        head_copy(out, out_hbm, sems_out, h).start()
+
+    for h in range(HC):
+        head(h)
+    finish_heads(out, out_hbm, sems_out)
 
 
 VM = pl.BlockSpec(memory_space=pltpu.VMEM)
 HBM = pl.BlockSpec(memory_space=pltpu.HBM)
-PARAMS = pltpu.CompilerParams(vmem_limit_bytes=20 * 1024 * 1024)
+PARAMS = pltpu.CompilerParams(vmem_limit_bytes=12 * 1024 * 1024)
 
 
 def call(kernel, outs, scratch, scal, *args, specs=None):
+    in_specs = [pl.BlockSpec(memory_space=pltpu.SMEM)] + (specs or [VM for _ in args])
+    out_specs = [VM if isinstance(out, jax.ShapeDtypeStruct) else HBM for out in outs]
     return pl.pallas_call(
         kernel,
         out_shape=outs,
-        in_specs=[pl.BlockSpec(memory_space=pltpu.SMEM)] + (specs or [VM for _ in args]),
-        out_specs=jax.tree.map(lambda _: VM, outs),
+        in_specs=in_specs,
+        out_specs=out_specs,
         scratch_shapes=scratch,
         compiler_params=PARAMS,
     )(scal, *args)
@@ -336,36 +369,47 @@
     qgnn = shift(qg[0], -2)
     qgn = swap(raw)
     tiles = pltpu.VMEM((5, 2 * BLK, BLK), F32)
-    row_tiles = pltpu.VMEM((7, 2 * BLK, BLK), F32)
+    row_tiles = pltpu.VMEM((2, 7, 2 * BLK, BLK), F32)
     cols = pltpu.VMEM((2 * BLK, BLK), F32)
+    halo = pltpu.VMEM((SIDE, 2, HC, BLK, HD), BF)
+    sems = pltpu.SemaphoreType.DMA((HC,))
     part_shape = (SIDE // 2, 2, HC, 2 * BLK, HD)
     dq_late, stats_late, part = call(
         early_kernel,
         [
             blocks_of(1, 2),
             jax.ShapeDtypeStruct((16, BLK), F32),
-            jax.ShapeDtypeStruct(part_shape, F32),
+            pltpu.HBM(part_shape, F32),
         ],
-        [cols, tiles, tiles, row_tiles, row_tiles],
-        scal, qg, kv, kvp,
+        [
+            cols, tiles, tiles, row_tiles, row_tiles, halo,
+            pltpu.VMEM(part_shape, F32), sems, sems,
+        ],
+        scal, qg, kv, in_hbm(kvp),
+        specs=[VM, VM, HBM],
     )
     dq, stats, front = call(
         query_kernel,
         [
-            blocks_of(1),
+            pltpu.HBM(blocks_of(1).shape, BF),
             jax.ShapeDtypeStruct((8 * SIDE, BLK), F32),
             jax.ShapeDtypeStruct((8, BLK), F32),
         ],
-        [cols, tiles, row_tiles, row_tiles],
-        scal, qg, kv, kvp, kvpp, dq_late, stats_late,
+        [cols, tiles, row_tiles, row_tiles, halo, pltpu.VMEM(blocks_of(1).shape, BF), sems, sems],
+        scal, qg, kv, in_hbm(kvp), kvpp, dq_late, stats_late,
+        specs=[VM, VM, HBM, VM, VM, VM],
     )
     near = shift(stats, -1)
     after = shift(front, -2)
-    back = swap(in_hbm(dq))
+    back = swap(dq)
     (query_grad,) = unpack(back)
-    dkv = call(
-        far_key_kernel, blocks_of(2),
-        [tiles, pltpu.VMEM(part_shape, F32), pltpu.SemaphoreType.DMA(())],
+    (dkv,) = call(
+        far_key_kernel,
+        [pltpu.HBM(blocks_of(2).shape, BF)],
+        [
+            tiles, pltpu.VMEM(part_shape, F32), pltpu.VMEM(blocks_of(2).shape, BF),
+            sems, sems,
+        ],
         scal, qg, qgn, qgnn, kv, stats, near, after, in_hbm(part),
         specs=[VM] * 7 + [HBM],
     )

time: 125 us -> 124 us (level)
  the two profiles are of different devices: /device:TPU:1 before, /device:TPU:32 now
where the time goes in v3:
time: 124 us; the launch traced here: 123 us
  waiting for transfers between devices  54.4 us (44%)
  starting transfers between devices  37.4 us (30%)
  Pallas kernels  28.4 us (23%)
  between operations  1.59 us (1%)
    all_to_all x5, waiting for transfers between devices, swap(): return lax.all_to_all(value, INSIDE, 0, 0)  33.6 us
    ppermute x6, waiting for transfers between devices, shift(): return lax.ppermute(value, GROUPS, pairs)  20.8 us
    all_to_all x5, starting transfers between devices, swap(): return lax.all_to_all(value, INSIDE, 0, 0)  20.8 us
    pallas_call x3, Pallas kernels, call(): pl.pallas_call(kernel, out_shape=outs, in_specs=in_specs, out_specs=out_s...  20.3 us
    ppermute x6, starting transfers between devices, shift(): return lax.ppermute(value, GROUPS, pairs)  16.7 us
    pallas_call x2, Pallas kernels, pack(): pl.pallas_call(pack_kernel, out_shape=blocks_of(2), in_specs=[HBM, HBM],...  4.92 us
    pallas_call x2, Pallas kernels, unpack(): pl.pallas_call(unpack_kernel, out_shape=[rows] * arrays, in_specs=[VM], o...  3.18 us
  transfers between devices with their start and end apart: 11, of which 7 were waited for; matrix products, arithmetic and copies ran while one was open for 1% of the time, Pallas kernels for 20%

profile of v3, /device:TPU:32, one launch (start us, length us, event | category | flops | bytes accessed | tf_op | source)
XLA Modules:
  0.0 122.6 jit_solution(11263183695901633539)
XLA Ops:
  0.6 2.5 %shard_map.77 = bf16[4,2,4,128,128]{4,3,2,1,0:T(8,128)(2,1)} custom-call(bf16[128,2048]{1,0:T(8,128)(2,1)} %first.3, bf16[128,2048]{1,0:T(8,128)(2,1)} %second.3), custom_call_target="tpu_custom_call" | custom-call | tf_op jit(solution)/shard_map/pallas_call | solution.py:326
  3.1 4.3 %all-to-all-start.1 = ((bf16[4,2,4,128,128]{4,3,2,1,0:T(8,128)(2,1)}), bf16[4,2,4,128,128]{4,3,2,1,0:T(8,128)(2,1)S(1)}, u32[]{:S(2)}, u32[]{:S(2)}) async-start(bf16[4,2,4,128,128]{4,3,2,1,0:T(8,128)(2,1)} %shard_map.77), calls=%async_computation.1 | async-start | bytes 2097152 | tf_op jit(solution)/shard_map/all_to_all | solution.py:356
  7.4 2.4 %shard_map.76 = bf16[4,2,4,128,128]{4,3,2,1,0:T(8,128)(2,1)} custom-call(bf16[128,2048]{1,0:T(8,128)(2,1)} %first.2, bf16[128,2048]{1,0:T(8,128)(2,1)} %second.2), custom_call_target="tpu_custom_call" | custom-call | tf_op jit(solution)/shard_map/pallas_call | solution.py:326
  9.9 3.0 %collective-permute-start.2 = (bf16[4,2,4,128,128]{4,3,2,1,0:T(8,128)(2,1)}, bf16[4,2,4,128,128]{4,3,2,1,0:T(8,128)(2,1)}, u32[]{:S(2)}, u32[]{:S(2)}) collective-permute-start(bf16[4,2,4,128,128]{4,3,2,1,0:T(8,128)(2,1)} %shard_map.76), channel_id=1, source_target_pairs={{4,0},{8,4},{12,8},{16,12},{20,16},{24,20},{28,24},{32,28},{36,32}... | collective-permute-start | bytes 3145736 | tf_op jit(solution)/shard_map/ppermute | solution.py:352
  12.8 9.7 %all-to-all-done.1.kv = bf16[4,2,4,128,128]{4,3,2,1,0:T(8,128)(2,1)S(1)} async-done(((bf16[4,2,4,128,128]{4,3,2,1,0:T(8,128)(2,1)}), bf16[4,2,4,128,128]{4,3,2,1,0:T(8,128)(2,1)S(1)}, u32[]{:S(2)}, u32[]{:S(2)}) %all-to-all-start.1) | async-done | bytes 1048608 | tf_op jit(solution)/shard_map/all_to_all | solution.py:356
  22.5 3.5 %all-to-all-start = ((bf16[4,2,4,128,128]{4,3,2,1,0:T(8,128)(2,1)}), bf16[4,2,4,128,128]{4,3,2,1,0:T(8,128)(2,1)S(1)}, u32[]{:S(2)}, u32[]{:S(2)}) async-start(bf16[4,2,4,128,128]{4,3,2,1,0:T(8,128)(2,1)} %shard_map.76), calls=%async_computation | async-start | bytes 2097152 | tf_op jit(solution)/shard_map/all_to_all | solution.py:356
  26.0 3.8 %collective-permute-start = (bf16[4,2,4,128,128]{4,3,2,1,0:T(8,128)(2,1)S(1)}, bf16[4,2,4,128,128]{4,3,2,1,0:T(8,128)(2,1)}, u32[]{:S(2)}, u32[]{:S(2)}) collective-permute-start(bf16[4,2,4,128,128]{4,3,2,1,0:T(8,128)(2,1)S(1)} %all-to-all-done.1.kv), channel_id=1, source_target_pairs={{0,4},{4,8},{8,12},{12,16},{16,20},{20,24},{24,28},{28,32},{32,36}... | collective-permute-start | bytes 3145736 | tf_op jit(solution)/shard_map/ppermute | solution.py:352
  29.9 10.4 %all-to-all-done.qg = bf16[4,2,4,128,128]{4,3,2,1,0:T(8,128)(2,1)S(1)} async-done(((bf16[4,2,4,128,128]{4,3,2,1,0:T(8,128)(2,1)}), bf16[4,2,4,128,128]{4,3,2,1,0:T(8,128)(2,1)S(1)}, u32[]{:S(2)}, u32[]{:S(2)}) %all-to-all-start) | async-done | bytes 1048608 | tf_op jit(solution)/shard_map/all_to_all | solution.py:356
  40.2 3.5 %all-to-all-start.3 = ((bf16[4,2,4,128,128]{4,3,2,1,0:T(8,128)(2,1)}), bf16[4,2,4,128,128]{4,3,2,1,0:T(8,128)(2,1)S(1)}, u32[]{:S(2)}, u32[]{:S(2)}) async-start(bf16[4,2,4,128,128]{4,3,2,1,0:T(8,128)(2,1)} %collective-permute-done.2), calls=%async_computation.3 | async-start | bytes 2097152 | tf_op jit(solution)/shard_map/all_to_all | solution.py:356
  44.5 5.2 %collective-permute-start.1 = (bf16[2,4,128,128]{3,2,1,0:T(8,128)(2,1)}, bf16[2,4,128,128]{3,2,1,0:T(8,128)(2,1)S(1)}, u32[]{:S(2)}, u32[]{:S(2)}) collective-permute-start(bf16[2,4,128,128]{3,2,1,0:T(8,128)(2,1)} %slice_bitcast_fusion.1), channel_id=1, source_target_pairs={{0,8},{4,12},{8,16},{12,20},{16,24},{20,28},{24,32},{28,36},{32,40... | collective-permute-start | bytes 786440 | tf_op jit(solution)/shard_map/ppermute | solution.py:352
  50.4 8.5 %collective-permute-done.kvp_hbm = bf16[4,2,4,128,128]{4,3,2,1,0:T(8,128)(2,1)} collective-permute-done((bf16[4,2,4,128,128]{4,3,2,1,0:T(8,128)(2,1)S(1)}, bf16[4,2,4,128,128]{4,3,2,1,0:T(8,128)(2,1)}, u32[]{:S(2)}, u32[]{:S(2)}) %collective-permute-start) | collective-permute-done | bytes 1048608 | tf_op jit(solution)/shard_map/ppermute | solution.py:352
  58.9 7.1 %shard_map.78 = (bf16[2,1,4,128,128]{4,3,2,1,0:T(8,128)(2,1)S(1)}, f32[16,128]{1,0:T(8,128)S(1)}, f32[2,2,4,256,128]{4,3,2,1,0:T(8,128)}) custom-call(s32[2]{0:T(128)S(1)} %pad_add_fusion.scal, bf16[4,2,4,128,128]{4,3,2,1,0:T(8,128)(2,1)S(1)} %all-to-all-done.qg, bf16[4,2,4,128,128]{4,3,2,1,0:T(8,128)(2,1)S(1)} %all-to-all-done.1.kv, ...), custom_call_target="tpu_custom_call" | custom-call | tf_op jit(solution)/shard_map/pallas_call | solution.py:307
  66.0 5.3 %shard_map.79 = (bf16[4,1,4,128,128]{4,3,2,1,0:T(8,128)(2,1)}, f32[32,128]{1,0:T(8,128)S(1)}, f32[8,128]{1,0:T(8,128)S(1)}) custom-call(s32[2]{0:T(128)S(1)} %pad_add_fusion.scal, bf16[4,2,4,128,128]{4,3,2,1,0:T(8,128)(2,1)S(1)} %all-to-all-done.qg, bf16[4,2,4,128,128]{4,3,2,1,0:T(8,128)(2,1)S(1)} %all-to-all-done.1.kv, ...), custom_call_target="tpu_custom_call" | custom-call | tf_op jit(solution)/shard_map/pallas_call | solution.py:307
  71.2 4.9 %all-to-all-start.2 = ((bf16[4,1,4,128,128]{4,3,2,1,0:T(8,128)(2,1)}), bf16[4,1,4,128,128]{4,3,2,1,0:T(8,128)(2,1)}, u32[]{:S(2)}, u32[]{:S(2)}) async-start(bf16[4,1,4,128,128]{4,3,2,1,0:T(8,128)(2,1)} %get-tuple-element.13), calls=%async_computation.2 | async-start | bytes 1048576 | tf_op jit(solution)/shard_map/all_to_all | solution.py:356
  76.2 1.3 %collective-permute-start.3 = (bf16[2,4,128,128]{3,2,1,0:T(8,128)(2,1)S(1)}, bf16[2,4,128,128]{3,2,1,0:T(8,128)(2,1)S(1)}, u32[]{:S(2)}, u32[]{:S(2)}) collective-permute-start(bf16[2,4,128,128]{3,2,1,0:T(8,128)(2,1)S(1)} %slice_bitcast_fusion), channel_id=1, source_target_pairs={{8,0},{12,4},{16,8},{20,12},{24,16},{28,20},{32,24},{36,28},{40,32... | collective-permute-start | bytes 786440 | tf_op jit(solution)/shard_map/ppermute | solution.py:352
  77.5 1.9 %collective-permute-start.4 = (f32[32,128]{1,0:T(8,128)S(1)}, f32[32,128]{1,0:T(8,128)S(1)}, u32[]{:S(2)}, u32[]{:S(2)}) collective-permute-start(f32[32,128]{1,0:T(8,128)S(1)} %get-tuple-element.14.stats), channel_id=1, source_target_pairs={{4,0},{8,4},{12,8},{16,12},{20,16},{24,20},{28,24},{32,28},{36,32}... | collective-permute-start | bytes 49160 | tf_op jit(solution)/shard_map/ppermute | solution.py:352
  79.4 1.5 %collective-permute-start.5 = (f32[8,128]{1,0:T(8,128)S(1)}, f32[8,128]{1,0:T(8,128)S(1)}, u32[]{:S(2)}, u32[]{:S(2)}) collective-permute-start(f32[8,128]{1,0:T(8,128)S(1)} %get-tuple-element.15), channel_id=1, source_target_pairs={{8,0},{12,4},{16,8},{20,12},{24,16},{28,20},{32,24},{36,28},{40,32... | collective-permute-start | bytes 12296 | tf_op jit(solution)/shard_map/ppermute | solution.py:352
  80.9 7.8 %collective-permute-done.3.qgnn = bf16[2,4,128,128]{3,2,1,0:T(8,128)(2,1)S(1)} collective-permute-done((bf16[2,4,128,128]{3,2,1,0:T(8,128)(2,1)S(1)}, bf16[2,4,128,128]{3,2,1,0:T(8,128)(2,1)S(1)}, u32[]{:S(2)}, u32[]{:S(2)}) %collective-permute-start.3) | collective-permute-done | bytes 262176 | tf_op jit(solution)/shard_map/ppermute | solution.py:352
  88.9 4.3 %collective-permute-done.4.near = f32[32,128]{1,0:T(8,128)S(1)} collective-permute-done((f32[32,128]{1,0:T(8,128)S(1)}, f32[32,128]{1,0:T(8,128)S(1)}, u32[]{:S(2)}, u32[]{:S(2)}) %collective-permute-start.4) | collective-permute-done | bytes 16416 | tf_op jit(solution)/shard_map/ppermute | solution.py:352
  93.3 7.9 %shard_map.81 = bf16[4,2,4,128,128]{4,3,2,1,0:T(8,128)(2,1)} custom-call(s32[2]{0:T(128)S(1)} %pad_add_fusion.scal, bf16[4,2,4,128,128]{4,3,2,1,0:T(8,128)(2,1)S(1)} %all-to-all-done.qg, bf16[4,2,4,128,128]{4,3,2,1,0:T(8,128)(2,1)S(1)} %all-to-all-done.3.qgn, bf16[2,4,128,128]{3,2,1,0:T(8,128)(2,1)S(1)} %collective-permute-done.3.qgnn, ...), custom_call_target="tpu_custom_call" | custom-call | tf_op jit(solution)/shard_map/pallas_call | solution.py:307
  101.2 4.5 %all-to-all-start.4 = ((bf16[4,2,4,128,128]{4,3,2,1,0:T(8,128)(2,1)}), bf16[4,2,4,128,128]{4,3,2,1,0:T(8,128)(2,1)S(1)}, u32[]{:S(2)}, u32[]{:S(2)}) async-start(bf16[4,2,4,128,128]{4,3,2,1,0:T(8,128)(2,1)} %shard_map.81), calls=%async_computation.4 | async-start | bytes 2097152 | tf_op jit(solution)/shard_map/all_to_all | solution.py:356
  105.7 2.0 %shard_map.80 = bf16[128,2048]{1,0:T(8,128)(2,1)} custom-call(bf16[4,1,4,128,128]{4,3,2,1,0:T(8,128)(2,1)} %all-to-all-done.2.back), custom_call_target="tpu_custom_call" | custom-call | tf_op jit(solution)/shard_map/pallas_call | solution.py:339
  107.7 13.5 %all-to-all-done.4.back = bf16[4,2,4,128,128]{4,3,2,1,0:T(8,128)(2,1)S(1)} async-done(((bf16[4,2,4,128,128]{4,3,2,1,0:T(8,128)(2,1)}), bf16[4,2,4,128,128]{4,3,2,1,0:T(8,128)(2,1)S(1)}, u32[]{:S(2)}, u32[]{:S(2)}) %all-to-all-start.4) | async-done | bytes 1048608 | tf_op jit(solution)/shard_map/all_to_all | solution.py:356
  121.2 1.2 shard_map.82
  (8 shorter events, 1.0 us)
Async XLA Ops:
  3.1 19.4 %all-to-all-start.1 = ((bf16[4,2,4,128,128]{4,3,2,1,0:T(8,128)(2,1)}), bf16[4,2,4,128,128]{4,3,2,1,0:T(8,128)(2,1)S(1)}, u32[]{:S(2)}, u32[]{:S(2)}) async-start(bf16[4,2,4,128,128]{4,3,2,1,0:T(8,128)(2,1)} %shard_map.77), calls=%async_computation.1 | async-start | bytes 2097152 | tf_op jit(solution)/shard_map/all_to_all | solution.py:356
  9.9 30.4 %collective-permute-start.2 = (bf16[4,2,4,128,128]{4,3,2,1,0:T(8,128)(2,1)}, bf16[4,2,4,128,128]{4,3,2,1,0:T(8,128)(2,1)}, u32[]{:S(2)}, u32[]{:S(2)}) collective-permute-start(bf16[4,2,4,128,128]{4,3,2,1,0:T(8,128)(2,1)} %shard_map.76), channel_id=1, source_target_pairs={{4,0},{8,4},{12,8},{16,12},{20,16},{24,20},{28,24},{32,28},{36,32}... | collective-permute-start | bytes 3145736 | tf_op jit(solution)/shard_map/ppermute | solution.py:352
  22.5 17.7 %all-to-all-start = ((bf16[4,2,4,128,128]{4,3,2,1,0:T(8,128)(2,1)}), bf16[4,2,4,128,128]{4,3,2,1,0:T(8,128)(2,1)S(1)}, u32[]{:S(2)}, u32[]{:S(2)}) async-start(bf16[4,2,4,128,128]{4,3,2,1,0:T(8,128)(2,1)} %shard_map.76), calls=%async_computation | async-start | bytes 2097152 | tf_op jit(solution)/shard_map/all_to_all | solution.py:356
  26.0 32.8 %collective-permute-start = (bf16[4,2,4,128,128]{4,3,2,1,0:T(8,128)(2,1)S(1)}, bf16[4,2,4,128,128]{4,3,2,1,0:T(8,128)(2,1)}, u32[]{:S(2)}, u32[]{:S(2)}) collective-permute-start(bf16[4,2,4,128,128]{4,3,2,1,0:T(8,128)(2,1)S(1)} %all-to-all-done.1.kv), channel_id=1, source_target_pairs={{0,4},{4,8},{8,12},{12,16},{16,20},{20,24},{24,28},{28,32},{32,36}... | collective-permute-start | bytes 3145736 | tf_op jit(solution)/shard_map/ppermute | solution.py:352
  40.2 31.0 %all-to-all-start.3 = ((bf16[4,2,4,128,128]{4,3,2,1,0:T(8,128)(2,1)}), bf16[4,2,4,128,128]{4,3,2,1,0:T(8,128)(2,1)S(1)}, u32[]{:S(2)}, u32[]{:S(2)}) async-start(bf16[4,2,4,128,128]{4,3,2,1,0:T(8,128)(2,1)} %collective-permute-done.2), calls=%async_computation.3 | async-start | bytes 2097152 | tf_op jit(solution)/shard_map/all_to_all | solution.py:356
  44.5 21.5 %collective-permute-start.1 = (bf16[2,4,128,128]{3,2,1,0:T(8,128)(2,1)}, bf16[2,4,128,128]{3,2,1,0:T(8,128)(2,1)S(1)}, u32[]{:S(2)}, u32[]{:S(2)}) collective-permute-start(bf16[2,4,128,128]{3,2,1,0:T(8,128)(2,1)} %slice_bitcast_fusion.1), channel_id=1, source_target_pairs={{0,8},{4,12},{8,16},{12,20},{16,24},{20,28},{24,32},{28,36},{32,40... | collective-permute-start | bytes 786440 | tf_op jit(solution)/shard_map/ppermute | solution.py:352
  71.2 30.0 %all-to-all-start.2 = ((bf16[4,1,4,128,128]{4,3,2,1,0:T(8,128)(2,1)}), bf16[4,1,4,128,128]{4,3,2,1,0:T(8,128)(2,1)}, u32[]{:S(2)}, u32[]{:S(2)}) async-start(bf16[4,1,4,128,128]{4,3,2,1,0:T(8,128)(2,1)} %get-tuple-element.13), calls=%async_computation.2 | async-start | bytes 1048576 | tf_op jit(solution)/shard_map/all_to_all | solution.py:356
  76.2 12.5 %collective-permute-start.3 = (bf16[2,4,128,128]{3,2,1,0:T(8,128)(2,1)S(1)}, bf16[2,4,128,128]{3,2,1,0:T(8,128)(2,1)S(1)}, u32[]{:S(2)}, u32[]{:S(2)}) collective-permute-start(bf16[2,4,128,128]{3,2,1,0:T(8,128)(2,1)S(1)} %slice_bitcast_fusion), channel_id=1, source_target_pairs={{8,0},{12,4},{16,8},{20,12},{24,16},{28,20},{32,24},{36,28},{40,32... | collective-permute-start | bytes 786440 | tf_op jit(solution)/shard_map/ppermute | solution.py:352
  77.5 15.8 %collective-permute-start.4 = (f32[32,128]{1,0:T(8,128)S(1)}, f32[32,128]{1,0:T(8,128)S(1)}, u32[]{:S(2)}, u32[]{:S(2)}) collective-permute-start(f32[32,128]{1,0:T(8,128)S(1)} %get-tuple-element.14.stats), channel_id=1, source_target_pairs={{4,0},{8,4},{12,8},{16,12},{20,16},{24,20},{28,24},{32,28},{36,32}... | collective-permute-start | bytes 49160 | tf_op jit(solution)/shard_map/ppermute | solution.py:352
  79.4 9.5 %collective-permute-start.5 = (f32[8,128]{1,0:T(8,128)S(1)}, f32[8,128]{1,0:T(8,128)S(1)}, u32[]{:S(2)}, u32[]{:S(2)}) collective-permute-start(f32[8,128]{1,0:T(8,128)S(1)} %get-tuple-element.15), channel_id=1, source_target_pairs={{8,0},{12,4},{16,8},{20,12},{24,16},{28,20},{32,24},{36,28},{40,32... | collective-permute-start | bytes 12296 | tf_op jit(solution)/shard_map/ppermute | solution.py:352
  101.2 20.0 %all-to-all-start.4 = ((bf16[4,2,4,128,128]{4,3,2,1,0:T(8,128)(2,1)}), bf16[4,2,4,128,128]{4,3,2,1,0:T(8,128)(2,1)S(1)}, u32[]{:S(2)}, u32[]{:S(2)}) async-start(bf16[4,2,4,128,128]{4,3,2,1,0:T(8,128)(2,1)} %shard_map.81), calls=%async_computation.4 | async-start | bytes 2097152 | tf_op jit(solution)/shard_map/all_to_all | solution.py:356

commit v4 on v3

--- a/solution.py
+++ b/solution.py
@@ -78,7 +78,7 @@
 
 
 A_TILES = (5, 4, 3, 0, -1)
-A_STEPS = ((0, 1), (2, 3), (4, 5), (6,))
+A_STEPS = ((6,), (4, 5), (2, 3), (0, 1))
 
 
 def fill_a(width, bias):
@@ -86,13 +86,15 @@
         bias[at] = mask_tile(width, blocks, (2 * BLK, BLK), 0)
 
 
-def query_half(j, h, group, qg, keys, bias, wts, prods, cols):
+def query_half(j, h, group, qg, keys, bias, wts, prods, cols, arrived):
     shape = (2 * BLK, BLK)
     query = joined([qg[j, 0, h], qg[j + 1, 0, h]])
     grad = joined([qg[j, 1, h], qg[j + 1, 1, h]])
     norm = jnp.zeros(shape, F32)
     centre = jnp.zeros(shape, F32)
     for steps in A_STEPS:
+        if j + steps[0] <= SIDE < j + steps[0] + 2:
+            arrived(h)
         logits2 = dot(query, joined([keys(j + s, 0, h) for s in steps]), NT)
         product2 = dot(grad, joined([keys(j + s, 1, h) for s in steps]), NT)
         for part, step in enumerate(steps):
@@ -159,14 +161,18 @@
         return kvp[at - 1, which, h] if at <= SIDE else kv[at - SIDE - 1, which, h]
 
     def head(h):
-        arrived(h)
-        total = query_half(2, h, scal[1], qg, keys, bias, wts, prods, cols)
+        total = query_half(2, h, scal[1], qg, keys, bias, wts, prods, cols, arrived)
         dq[0, 0, h] = total[:BLK]
         dq[1, 0, h] = total[BLK:]
 
     for h in range(HC):
         head(h)
     stats[:8], stats[8:] = rows_of(cols)
+
+    def leave(half, h):
+        return pltpu.make_async_copy(
+            part.at[half, :, h], part_hbm.at[half, :, h], sems_out.at[half, h]
+        )
 
     def key_head(h):
         for half, steps in ((0, (2, 3)), (1, (0, 1))):
@@ -182,17 +188,21 @@
             )
             part[half, 0, h] = dk
             part[half, 1, h] = dv
-        head_copy(part, part_hbm, sems_out, h).start()
+            leave(half, h).start()
 
     for h in range(HC):
         key_head(h)
-    finish_heads(part, part_hbm, sems_out)
+    for h in range(HC):
+        for half in range(2):
+            leave(half, h).wait()
 
 
 def query_kernel(
-    scal, qg, kv, kvp_hbm, kvpp, dq_late, stats_late, dq_hbm, stats, front,
-    cols, bias, wts, prods, kvp, dq_own, sems, sems_out,
+    scal, qg, kv, kvp_hbm, kvpp_hbm, dq_late, stats_late, dq_hbm, stats, front,
+    cols, bias, wts, prods, kvp, kvpp, dq_own, sem, sems, sems_out,
 ):
+    fetch = pltpu.make_async_copy(kvpp_hbm, kvpp, sem)
+    fetch.start()
     arrived = fetch_heads(kvp_hbm, kvp, sems)
     fill_a(scal[0], bias)
     cols[...] = jnp.zeros_like(cols)
@@ -205,8 +215,10 @@
         return kvp[at - 1, which, h] if at <= SIDE else kv[at - SIDE - 1, which, h]
 
     def head(h):
-        arrived(h)
-        total = query_half(0, h, scal[1], qg, keys, bias, wts, prods, cols)
+        total = query_half(
+            0, h, scal[1], qg, keys, bias, wts, prods, cols,
+            lambda h: (arrived(h), fetch.wait() if h == 0 else None),
+        )
         dq_own[0, 0, h] = total[:BLK]
         dq_own[1, 0, h] = total[BLK:]
         head_copy(dq_own, dq_hbm, sems_out, h).start()
@@ -272,19 +284,21 @@
         return stats_rows(after, 0, h) if at == 2 * SIDE else stats_rows(near, at - SIDE, h)
 
     def head(h):
-        arrived(h)
         for half, todo in ((0, ((0, 1), (4, 5), (6,))), (1, ((2, 3), (4, 5), (6,)))):
             j = 2 * half
+            zero = jnp.zeros((2 * BLK, HD), F32)
             dk, dv = key_half(
                 todo,
                 joined([kv[j, 0, h], kv[j + 1, 0, h]]),
                 joined([kv[j, 1, h], kv[j + 1, 1, h]]),
                 lambda s, which: queries(j + s, which, h),
                 lambda s: stats_of(j + s, h),
-                bias, part[half, 0, h], part[half, 1, h],
+                bias, zero, zero,
             )
-            dk = (dk * SCALE).astype(BF)
-            dv = dv.astype(BF)
+            if half == 0:
+                arrived(h)
+            dk = ((dk + part[half, 0, h]) * SCALE).astype(BF)
+            dv = (dv + part[half, 1, h]).astype(BF)
             out[j, 0, h] = dk[:BLK]
             out[j + 1, 0, h] = dk[BLK:]
             out[j, 1, h] = dv[:BLK]
@@ -383,7 +397,7 @@
         ],
         [
             cols, tiles, tiles, row_tiles, row_tiles, halo,
-            pltpu.VMEM(part_shape, F32), sems, sems,
+            pltpu.VMEM(part_shape, F32), sems, pltpu.SemaphoreType.DMA((2, HC)),
         ],
         scal, qg, kv, in_hbm(kvp),
         specs=[VM, VM, HBM],
@@ -395,9 +409,13 @@
             jax.ShapeDtypeStruct((8 * SIDE, BLK), F32),
             jax.ShapeDtypeStruct((8, BLK), F32),
         ],
-        [cols, tiles, row_tiles, row_tiles, halo, pltpu.VMEM(blocks_of(1).shape, BF), sems, sems],
-        scal, qg, kv, in_hbm(kvp), kvpp, dq_late, stats_late,
-        specs=[VM, VM, HBM, VM, VM, VM],
+        [
+            cols, tiles, row_tiles, row_tiles, halo,
+            pltpu.VMEM((2, HC, BLK, HD), BF), pltpu.VMEM(blocks_of(1).shape, BF),
+            pltpu.SemaphoreType.DMA(()), sems, sems,
+        ],
+        scal, qg, kv, in_hbm(kvp), in_hbm(kvpp), dq_late, stats_late,
+        specs=[VM, VM, HBM, HBM, VM, VM],
     )
     near = shift(stats, -1)
     after = shift(front, -2)

time: 124 us -> 122 us (0.984)
  Pallas kernels: 28.4 us -> 26.8 us
    pallas_call x3, Pallas kernels: 20.3 us -> 18.7 us  [call(): pl.pallas_call(kernel, out_shape=outs, in_specs=in_specs, out_specs=out_s...]
  transfers between devices with their start and end apart: 11 -> 11, of which waited for: 7 -> 7; matrix products, arithmetic and copies ran while one was open for 1% -> 0% of each run, Pallas kernels for 20% -> 19%
where the time goes in v4:
time: 122 us; the launch traced here: 121 us
  waiting for transfers between devices  54.4 us (45%)
  starting transfers between devices  38.1 us (31%)
  Pallas kernels  26.8 us (22%)
  between operations  1.59 us (1%)
    all_to_all x5, waiting for transfers between devices, swap(): return lax.all_to_all(value, INSIDE, 0, 0)  33.5 us
    ppermute x6, waiting for transfers between devices, shift(): return lax.ppermute(value, GROUPS, pairs)  20.9 us
    all_to_all x5, starting transfers between devices, swap(): return lax.all_to_all(value, INSIDE, 0, 0)  20.7 us
    pallas_call x3, Pallas kernels, call(): pl.pallas_call(kernel, out_shape=outs, in_specs=in_specs, out_specs=out_s...  18.7 us
    ppermute x6, starting transfers between devices, shift(): return lax.ppermute(value, GROUPS, pairs)  17.4 us
    pallas_call x2, Pallas kernels, pack(): pl.pallas_call(pack_kernel, out_shape=blocks_of(2), in_specs=[HBM, HBM],...  4.92 us
    pallas_call x2, Pallas kernels, unpack(): pl.pallas_call(unpack_kernel, out_shape=[rows] * arrays, in_specs=[VM], o...  3.18 us
  transfers between devices with their start and end apart: 11, of which 7 were waited for; matrix products, arithmetic and copies ran while one was open for 0% of the time, Pallas kernels for 19%

profile of v4, /device:TPU:32, one launch (start us, length us, event | category | flops | bytes accessed | tf_op | source)
XLA Modules:
  0.0 121.0 jit_solution(8414283152275961591)
XLA Ops:
  0.6 2.5 %shard_map.77 = bf16[4,2,4,128,128]{4,3,2,1,0:T(8,128)(2,1)} custom-call(bf16[128,2048]{1,0:T(8,128)(2,1)} %first.3, bf16[128,2048]{1,0:T(8,128)(2,1)} %second.3), custom_call_target="tpu_custom_call" | custom-call | tf_op jit(solution)/shard_map/pallas_call | solution.py:340
  3.1 4.3 %all-to-all-start.1 = ((bf16[4,2,4,128,128]{4,3,2,1,0:T(8,128)(2,1)}), bf16[4,2,4,128,128]{4,3,2,1,0:T(8,128)(2,1)S(1)}, u32[]{:S(2)}, u32[]{:S(2)}) async-start(bf16[4,2,4,128,128]{4,3,2,1,0:T(8,128)(2,1)} %shard_map.77), calls=%async_computation.1 | async-start | bytes 2097152 | tf_op jit(solution)/shard_map/all_to_all | solution.py:370
  7.4 2.4 %shard_map.76 = bf16[4,2,4,128,128]{4,3,2,1,0:T(8,128)(2,1)} custom-call(bf16[128,2048]{1,0:T(8,128)(2,1)} %first.2, bf16[128,2048]{1,0:T(8,128)(2,1)} %second.2), custom_call_target="tpu_custom_call" | custom-call | tf_op jit(solution)/shard_map/pallas_call | solution.py:340
  9.9 3.0 %collective-permute-start.2 = (bf16[4,2,4,128,128]{4,3,2,1,0:T(8,128)(2,1)}, bf16[4,2,4,128,128]{4,3,2,1,0:T(8,128)(2,1)}, u32[]{:S(2)}, u32[]{:S(2)}) collective-permute-start(bf16[4,2,4,128,128]{4,3,2,1,0:T(8,128)(2,1)} %shard_map.76), channel_id=1, source_target_pairs={{4,0},{8,4},{12,8},{16,12},{20,16},{24,20},{28,24},{32,28},{36,32}... | collective-permute-start | bytes 3145736 | tf_op jit(solution)/shard_map/ppermute | solution.py:366
  12.8 9.7 %all-to-all-done.1.kv = bf16[4,2,4,128,128]{4,3,2,1,0:T(8,128)(2,1)S(1)} async-done(((bf16[4,2,4,128,128]{4,3,2,1,0:T(8,128)(2,1)}), bf16[4,2,4,128,128]{4,3,2,1,0:T(8,128)(2,1)S(1)}, u32[]{:S(2)}, u32[]{:S(2)}) %all-to-all-start.1) | async-done | bytes 1048608 | tf_op jit(solution)/shard_map/all_to_all | solution.py:370
  22.5 3.5 %all-to-all-start = ((bf16[4,2,4,128,128]{4,3,2,1,0:T(8,128)(2,1)}), bf16[4,2,4,128,128]{4,3,2,1,0:T(8,128)(2,1)S(1)}, u32[]{:S(2)}, u32[]{:S(2)}) async-start(bf16[4,2,4,128,128]{4,3,2,1,0:T(8,128)(2,1)} %shard_map.76), calls=%async_computation | async-start | bytes 2097152 | tf_op jit(solution)/shard_map/all_to_all | solution.py:370
  26.0 3.8 %collective-permute-start = (bf16[4,2,4,128,128]{4,3,2,1,0:T(8,128)(2,1)S(1)}, bf16[4,2,4,128,128]{4,3,2,1,0:T(8,128)(2,1)}, u32[]{:S(2)}, u32[]{:S(2)}) collective-permute-start(bf16[4,2,4,128,128]{4,3,2,1,0:T(8,128)(2,1)S(1)} %all-to-all-done.1.kv), channel_id=1, source_target_pairs={{0,4},{4,8},{8,12},{12,16},{16,20},{20,24},{24,28},{28,32},{32,36}... | collective-permute-start | bytes 3145736 | tf_op jit(solution)/shard_map/ppermute | solution.py:366
  29.9 10.4 %all-to-all-done.qg = bf16[4,2,4,128,128]{4,3,2,1,0:T(8,128)(2,1)S(1)} async-done(((bf16[4,2,4,128,128]{4,3,2,1,0:T(8,128)(2,1)}), bf16[4,2,4,128,128]{4,3,2,1,0:T(8,128)(2,1)S(1)}, u32[]{:S(2)}, u32[]{:S(2)}) %all-to-all-start) | async-done | bytes 1048608 | tf_op jit(solution)/shard_map/all_to_all | solution.py:370
  40.2 3.5 %all-to-all-start.3 = ((bf16[4,2,4,128,128]{4,3,2,1,0:T(8,128)(2,1)}), bf16[4,2,4,128,128]{4,3,2,1,0:T(8,128)(2,1)S(1)}, u32[]{:S(2)}, u32[]{:S(2)}) async-start(bf16[4,2,4,128,128]{4,3,2,1,0:T(8,128)(2,1)} %collective-permute-done.2), calls=%async_computation.3 | async-start | bytes 2097152 | tf_op jit(solution)/shard_map/all_to_all | solution.py:370
  43.8 5.9 %collective-permute-start.1 = (bf16[2,4,128,128]{3,2,1,0:T(8,128)(2,1)S(1)}, bf16[2,4,128,128]{3,2,1,0:T(8,128)(2,1)}, u32[]{:S(2)}, u32[]{:S(2)}) collective-permute-start(bf16[2,4,128,128]{3,2,1,0:T(8,128)(2,1)S(1)} %slice_bitcast_fusion.1), channel_id=1, source_target_pairs={{0,8},{4,12},{8,16},{12,20},{16,24},{20,28},{24,32},{28,36},{32,40... | collective-permute-start | bytes 786440 | tf_op jit(solution)/shard_map/ppermute | solution.py:366
  50.4 8.5 %collective-permute-done.kvp_hbm = bf16[4,2,4,128,128]{4,3,2,1,0:T(8,128)(2,1)} collective-permute-done((bf16[4,2,4,128,128]{4,3,2,1,0:T(8,128)(2,1)S(1)}, bf16[4,2,4,128,128]{4,3,2,1,0:T(8,128)(2,1)}, u32[]{:S(2)}, u32[]{:S(2)}) %collective-permute-start) | collective-permute-done | bytes 1048608 | tf_op jit(solution)/shard_map/ppermute | solution.py:366
  58.9 6.8 %shard_map.78 = (bf16[2,1,4,128,128]{4,3,2,1,0:T(8,128)(2,1)S(1)}, f32[16,128]{1,0:T(8,128)S(1)}, f32[2,2,4,256,128]{4,3,2,1,0:T(8,128)}) custom-call(s32[2]{0:T(128)S(1)} %pad_add_fusion.scal, bf16[4,2,4,128,128]{4,3,2,1,0:T(8,128)(2,1)S(1)} %all-to-all-done.qg, bf16[4,2,4,128,128]{4,3,2,1,0:T(8,128)(2,1)S(1)} %all-to-all-done.1.kv, ...), custom_call_target="tpu_custom_call" | custom-call | tf_op jit(solution)/shard_map/pallas_call | solution.py:321
  65.7 5.1 %shard_map.79 = (bf16[4,1,4,128,128]{4,3,2,1,0:T(8,128)(2,1)}, f32[32,128]{1,0:T(8,128)S(1)}, f32[8,128]{1,0:T(8,128)S(1)}) custom-call(s32[2]{0:T(128)S(1)} %pad_add_fusion.scal, bf16[4,2,4,128,128]{4,3,2,1,0:T(8,128)(2,1)S(1)} %all-to-all-done.qg, bf16[4,2,4,128,128]{4,3,2,1,0:T(8,128)(2,1)S(1)} %all-to-all-done.1.kv, ...), custom_call_target="tpu_custom_call" | custom-call | tf_op jit(solution)/shard_map/pallas_call | solution.py:321
  70.9 4.9 %all-to-all-start.2 = ((bf16[4,1,4,128,128]{4,3,2,1,0:T(8,128)(2,1)}), bf16[4,1,4,128,128]{4,3,2,1,0:T(8,128)(2,1)}, u32[]{:S(2)}, u32[]{:S(2)}) async-start(bf16[4,1,4,128,128]{4,3,2,1,0:T(8,128)(2,1)} %get-tuple-element.13), calls=%async_computation.2 | async-start | bytes 1048576 | tf_op jit(solution)/shard_map/all_to_all | solution.py:370
  75.8 1.3 %collective-permute-start.3 = (bf16[2,4,128,128]{3,2,1,0:T(8,128)(2,1)S(1)}, bf16[2,4,128,128]{3,2,1,0:T(8,128)(2,1)S(1)}, u32[]{:S(2)}, u32[]{:S(2)}) collective-permute-start(bf16[2,4,128,128]{3,2,1,0:T(8,128)(2,1)S(1)} %slice_bitcast_fusion), channel_id=1, source_target_pairs={{8,0},{12,4},{16,8},{20,12},{24,16},{28,20},{32,24},{36,28},{40,32... | collective-permute-start | bytes 786440 | tf_op jit(solution)/shard_map/ppermute | solution.py:366
  77.1 1.9 %collective-permute-start.4 = (f32[32,128]{1,0:T(8,128)S(1)}, f32[32,128]{1,0:T(8,128)S(1)}, u32[]{:S(2)}, u32[]{:S(2)}) collective-permute-start(f32[32,128]{1,0:T(8,128)S(1)} %get-tuple-element.14.stats), channel_id=1, source_target_pairs={{4,0},{8,4},{12,8},{16,12},{20,16},{24,20},{28,24},{32,28},{36,32}... | collective-permute-start | bytes 49160 | tf_op jit(solution)/shard_map/ppermute | solution.py:366
  79.0 1.5 %collective-permute-start.5 = (f32[8,128]{1,0:T(8,128)S(1)}, f32[8,128]{1,0:T(8,128)S(1)}, u32[]{:S(2)}, u32[]{:S(2)}) collective-permute-start(f32[8,128]{1,0:T(8,128)S(1)} %get-tuple-element.15), channel_id=1, source_target_pairs={{8,0},{12,4},{16,8},{20,12},{24,16},{28,20},{32,24},{36,28},{40,32... | collective-permute-start | bytes 12296 | tf_op jit(solution)/shard_map/ppermute | solution.py:366
  80.5 8.0 %collective-permute-done.3.qgnn = bf16[2,4,128,128]{3,2,1,0:T(8,128)(2,1)S(1)} collective-permute-done((bf16[2,4,128,128]{3,2,1,0:T(8,128)(2,1)S(1)}, bf16[2,4,128,128]{3,2,1,0:T(8,128)(2,1)S(1)}, u32[]{:S(2)}, u32[]{:S(2)}) %collective-permute-start.3) | collective-permute-done | bytes 262176 | tf_op jit(solution)/shard_map/ppermute | solution.py:366
  88.7 4.2 %collective-permute-done.4.near = f32[32,128]{1,0:T(8,128)S(1)} collective-permute-done((f32[32,128]{1,0:T(8,128)S(1)}, f32[32,128]{1,0:T(8,128)S(1)}, u32[]{:S(2)}, u32[]{:S(2)}) %collective-permute-start.4) | collective-permute-done | bytes 16416 | tf_op jit(solution)/shard_map/ppermute | solution.py:366
  92.9 6.7 %shard_map.81 = bf16[4,2,4,128,128]{4,3,2,1,0:T(8,128)(2,1)} custom-call(s32[2]{0:T(128)S(1)} %pad_add_fusion.scal, bf16[4,2,4,128,128]{4,3,2,1,0:T(8,128)(2,1)S(1)} %all-to-all-done.qg, bf16[4,2,4,128,128]{4,3,2,1,0:T(8,128)(2,1)S(1)} %all-to-all-done.3.qgn, bf16[2,4,128,128]{3,2,1,0:T(8,128)(2,1)S(1)} %collective-permute-done.3.qgnn, ...), custom_call_target="tpu_custom_call" | custom-call | tf_op jit(solution)/shard_map/pallas_call | solution.py:321
  99.7 4.5 %all-to-all-start.4 = ((bf16[4,2,4,128,128]{4,3,2,1,0:T(8,128)(2,1)}), bf16[4,2,4,128,128]{4,3,2,1,0:T(8,128)(2,1)S(1)}, u32[]{:S(2)}, u32[]{:S(2)}) async-start(bf16[4,2,4,128,128]{4,3,2,1,0:T(8,128)(2,1)} %shard_map.81), calls=%async_computation.4 | async-start | bytes 2097152 | tf_op jit(solution)/shard_map/all_to_all | solution.py:370
  104.1 2.0 %shard_map.80 = bf16[128,2048]{1,0:T(8,128)(2,1)} custom-call(bf16[4,1,4,128,128]{4,3,2,1,0:T(8,128)(2,1)} %all-to-all-done.2.back), custom_call_target="tpu_custom_call" | custom-call | tf_op jit(solution)/shard_map/pallas_call | solution.py:353
  106.1 13.5 %all-to-all-done.4.back = bf16[4,2,4,128,128]{4,3,2,1,0:T(8,128)(2,1)S(1)} async-done(((bf16[4,2,4,128,128]{4,3,2,1,0:T(8,128)(2,1)}), bf16[4,2,4,128,128]{4,3,2,1,0:T(8,128)(2,1)S(1)}, u32[]{:S(2)}, u32[]{:S(2)}) %all-to-all-start.4) | async-done | bytes 1048608 | tf_op jit(solution)/shard_map/all_to_all | solution.py:370
  119.6 1.2 %shard_map.82 = (bf16[128,2048]{1,0:T(8,128)(2,1)}, bf16[128,2048]{1,0:T(8,128)(2,1)}) custom-call(bf16[4,2,4,128,128]{4,3,2,1,0:T(8,128)(2,1)S(1)} %all-to-all-done.4.back), custom_call_target="tpu_custom_call" | custom-call | tf_op jit(solution)/shard_map/pallas_call | solution.py:353
  (8 shorter events, 0.3 us)
Async XLA Ops:
  3.1 19.4 %all-to-all-start.1 = ((bf16[4,2,4,128,128]{4,3,2,1,0:T(8,128)(2,1)}), bf16[4,2,4,128,128]{4,3,2,1,0:T(8,128)(2,1)S(1)}, u32[]{:S(2)}, u32[]{:S(2)}) async-start(bf16[4,2,4,128,128]{4,3,2,1,0:T(8,128)(2,1)} %shard_map.77), calls=%async_computation.1 | async-start | bytes 2097152 | tf_op jit(solution)/shard_map/all_to_all | solution.py:370
  9.9 30.4 %collective-permute-start.2 = (bf16[4,2,4,128,128]{4,3,2,1,0:T(8,128)(2,1)}, bf16[4,2,4,128,128]{4,3,2,1,0:T(8,128)(2,1)}, u32[]{:S(2)}, u32[]{:S(2)}) collective-permute-start(bf16[4,2,4,128,128]{4,3,2,1,0:T(8,128)(2,1)} %shard_map.76), channel_id=1, source_target_pairs={{4,0},{8,4},{12,8},{16,12},{20,16},{24,20},{28,24},{32,28},{36,32}... | collective-permute-start | bytes 3145736 | tf_op jit(solution)/shard_map/ppermute | solution.py:366
  22.5 17.7 %all-to-all-start = ((bf16[4,2,4,128,128]{4,3,2,1,0:T(8,128)(2,1)}), bf16[4,2,4,128,128]{4,3,2,1,0:T(8,128)(2,1)S(1)}, u32[]{:S(2)}, u32[]{:S(2)}) async-start(bf16[4,2,4,128,128]{4,3,2,1,0:T(8,128)(2,1)} %shard_map.76), calls=%async_computation | async-start | bytes 2097152 | tf_op jit(solution)/shard_map/all_to_all | solution.py:370
  26.0 32.8 %collective-permute-start = (bf16[4,2,4,128,128]{4,3,2,1,0:T(8,128)(2,1)S(1)}, bf16[4,2,4,128,128]{4,3,2,1,0:T(8,128)(2,1)}, u32[]{:S(2)}, u32[]{:S(2)}) collective-permute-start(bf16[4,2,4,128,128]{4,3,2,1,0:T(8,128)(2,1)S(1)} %all-to-all-done.1.kv), channel_id=1, source_target_pairs={{0,4},{4,8},{8,12},{12,16},{16,20},{20,24},{24,28},{28,32},{32,36}... | collective-permute-start | bytes 3145736 | tf_op jit(solution)/shard_map/ppermute | solution.py:366
  40.2 30.6 %all-to-all-start.3 = ((bf16[4,2,4,128,128]{4,3,2,1,0:T(8,128)(2,1)}), bf16[4,2,4,128,128]{4,3,2,1,0:T(8,128)(2,1)S(1)}, u32[]{:S(2)}, u32[]{:S(2)}) async-start(bf16[4,2,4,128,128]{4,3,2,1,0:T(8,128)(2,1)} %collective-permute-done.2), calls=%async_computation.3 | async-start | bytes 2097152 | tf_op jit(solution)/shard_map/all_to_all | solution.py:370
  43.8 21.9 %collective-permute-start.1 = (bf16[2,4,128,128]{3,2,1,0:T(8,128)(2,1)S(1)}, bf16[2,4,128,128]{3,2,1,0:T(8,128)(2,1)}, u32[]{:S(2)}, u32[]{:S(2)}) collective-permute-start(bf16[2,4,128,128]{3,2,1,0:T(8,128)(2,1)S(1)} %slice_bitcast_fusion.1), channel_id=1, source_target_pairs={{0,8},{4,12},{8,16},{12,20},{16,24},{20,28},{24,32},{28,36},{32,40... | collective-permute-start | bytes 786440 | tf_op jit(solution)/shard_map/ppermute | solution.py:366
  70.9 28.8 %all-to-all-start.2 = ((bf16[4,1,4,128,128]{4,3,2,1,0:T(8,128)(2,1)}), bf16[4,1,4,128,128]{4,3,2,1,0:T(8,128)(2,1)}, u32[]{:S(2)}, u32[]{:S(2)}) async-start(bf16[4,1,4,128,128]{4,3,2,1,0:T(8,128)(2,1)} %get-tuple-element.13), calls=%async_computation.2 | async-start | bytes 1048576 | tf_op jit(solution)/shard_map/all_to_all | solution.py:370
  75.8 12.7 %collective-permute-start.3 = (bf16[2,4,128,128]{3,2,1,0:T(8,128)(2,1)S(1)}, bf16[2,4,128,128]{3,2,1,0:T(8,128)(2,1)S(1)}, u32[]{:S(2)}, u32[]{:S(2)}) collective-permute-start(bf16[2,4,128,128]{3,2,1,0:T(8,128)(2,1)S(1)} %slice_bitcast_fusion), channel_id=1, source_target_pairs={{8,0},{12,4},{16,8},{20,12},{24,16},{28,20},{32,24},{36,28},{40,32... | collective-permute-start | bytes 786440 | tf_op jit(solution)/shard_map/ppermute | solution.py:366
  77.1 15.8 %collective-permute-start.4 = (f32[32,128]{1,0:T(8,128)S(1)}, f32[32,128]{1,0:T(8,128)S(1)}, u32[]{:S(2)}, u32[]{:S(2)}) collective-permute-start(f32[32,128]{1,0:T(8,128)S(1)} %get-tuple-element.14.stats), channel_id=1, source_target_pairs={{4,0},{8,4},{12,8},{16,12},{20,16},{24,20},{28,24},{32,28},{36,32}... | collective-permute-start | bytes 49160 | tf_op jit(solution)/shard_map/ppermute | solution.py:366
  79.0 9.7 %collective-permute-start.5 = (f32[8,128]{1,0:T(8,128)S(1)}, f32[8,128]{1,0:T(8,128)S(1)}, u32[]{:S(2)}, u32[]{:S(2)}) collective-permute-start(f32[8,128]{1,0:T(8,128)S(1)} %get-tuple-element.15), channel_id=1, source_target_pairs={{8,0},{12,4},{16,8},{20,12},{24,16},{28,20},{32,24},{36,28},{40,32... | collective-permute-start | bytes 12296 | tf_op jit(solution)/shard_map/ppermute | solution.py:366
  99.7 20.0 %all-to-all-start.4 = ((bf16[4,2,4,128,128]{4,3,2,1,0:T(8,128)(2,1)}), bf16[4,2,4,128,128]{4,3,2,1,0:T(8,128)(2,1)S(1)}, u32[]{:S(2)}, u32[]{:S(2)}) async-start(bf16[4,2,4,128,128]{4,3,2,1,0:T(8,128)(2,1)} %shard_map.81), calls=%async_computation.4 | async-start | bytes 2097152 | tf_op jit(solution)/shard_map/all_to_all | solution.py:370
